TPU v7x, 32 devices: a whole 2x2x4 slice. The times are simulated.
32 devices in a mesh: hist: 8 (over y, x, core), col: 4 (over z).
Axes of the slice: x: 2, y: 2, z: 4, core: 2. Of those that a mesh axis runs over, the one named last changes fastest.
Arguments:
- less_row: bfloat16 [2, 128, 128, 1024], P(None, None, 'col', 'hist'), may hold values from -1.796875 to 1.796875
- less_col: bfloat16 [2, 128, 128, 1024], P(None, None, 'col', 'hist'), may hold values from -1.796875 to 1.796875
- great_row: bfloat16 [2, 128, 128, 1024], P(None, None, 'col', 'hist'), may hold values from -1.796875 to 1.796875
- great_col: bfloat16 [2, 128, 128, 1024], P(None, None, 'col', 'hist'), may hold values from -1.796875 to 1.796875
- density: float32 [2, 128, 128], replicated, may hold values from -1.8 to 1.8
- hamiltonian: float32 [128, 128], replicated, may hold values from -0.5 to 0.5
Outputs:
- less_row_out: bfloat16 [2, 128, 128, 1024], P(None, None, 'col', 'hist')
- less_col_out: bfloat16 [2, 128, 128, 1024], P(None, None, 'col', 'hist')
- great_row_out: bfloat16 [2, 128, 128, 1024], P(None, None, 'col', 'hist')
- great_col_out: bfloat16 [2, 128, 128, 1024], P(None, None, 'col', 'hist')
- density_out: float32 [2, 128, 128], replicated
All inputs are finite; a program needn't handle non-finite values.
Results may differ from a plain program's by a relative error of at most 0.033.
Values may be sent and summed in bfloat16 or wider, within the bound.
No kernel may reach another device: no remote copies, remote signals or barrier semaphores. Data moves between devices by JAX's collectives and lax.ppermute only.
A program may use at most 128 MiB of HBM per device.

v0:
```python
import functools

import jax
import jax.numpy as jnp
from jax import lax
from jax.experimental import pallas as pl
from jax.experimental.pallas import tpu as pltpu
from jax.sharding import PartitionSpec as P


step_length = 0.1
mean_field = 2.0
coupling = 1.0

HIGH = lax.Precision.HIGHEST
SUBLANES = 8
GROUP = 8
SPAN = 256


def dot_high(a, b):
    return jnp.dot(a, b, precision=HIGH, preferred_element_type=jnp.float32)


def eye_mask(size):
    rows = lax.broadcasted_iota(jnp.int32, (size, size), 0)
    return rows == lax.broadcasted_iota(jnp.int32, (size, size), 1)


def inverse(matrix):
    size = matrix.shape[0]
    blocks = [matrix[p : p + SUBLANES] for p in range(0, size, SUBLANES)]
    rows = lax.broadcasted_iota(jnp.int32, (SUBLANES, size), 0)
    lanes = lax.broadcasted_iota(jnp.int32, (SUBLANES, size), 1)
    for p in range(len(blocks)):
        first = p * SUBLANES
        pivot_lanes = (lanes >= first) & (lanes < first + SUBLANES)

        def columns(block):
            return [jnp.broadcast_to(block[:, first + c : first + c + 1], (SUBLANES, size)) for c in range(SUBLANES)]

        pivot = columns(blocks[p])
        row_block = jnp.where(pivot_lanes, jnp.where(lanes == rows + first, 1.0, 0.0), blocks[p])
        for j in range(SUBLANES):

            def across(value):
                return jnp.broadcast_to(value[j : j + 1], (SUBLANES, size))

            scale = 1.0 / across(pivot[j])
            factor = pivot[j]

            def eliminate(value):
                top = across(value) * scale
                return jnp.where(rows == j, top, value - factor * top)

            row_block = eliminate(row_block)
            pivot = [eliminate(value) if c > j else value for c, value in enumerate(pivot)]
        spread = [jnp.broadcast_to(row_block[c : c + 1], (SUBLANES, size)) for c in range(SUBLANES)]
        order = list(range(p + 1, len(blocks))) + list(range(p))
        for q in order:
            total = jnp.where(pivot_lanes, 0.0, blocks[q])
            for c, column in enumerate(columns(blocks[q])):
                total = total - column * spread[c]
            blocks[q] = total
        blocks[p] = row_block
    return jnp.concatenate(blocks, axis=0)


def spread_rows(ref, row):
    ref[...] = jnp.broadcast_to(row.reshape(1, 1, row.shape[-1]), ref.shape)


def diagonal_row(matrix):
    return jnp.sum(jnp.where(eye_mask(matrix.shape[0]), matrix, 0.0), axis=0, keepdims=True)


def solve_kernel(rotates, levels_ref, ham_ref, *refs):
    size = ham_ref.shape[0]
    eye = eye_mask(size)
    level = levels_ref[0]
    for row in range(1, levels_ref.shape[0]):
        level = level + levels_ref[row]
    halved = (0.5 * step_length) * (ham_ref[...] + mean_field * jnp.where(eye, level, 0.0))
    identity = jnp.where(eye, 1.0, 0.0)
    solved = inverse(identity + dot_high(halved, halved))
    unit_real = 2.0 * solved - identity
    unit_imag = -2.0 * dot_high(solved, halved)
    low_real, low_imag = unit_real.astype(jnp.bfloat16), unit_imag.astype(jnp.bfloat16)
    if rotates:
        rho_ref, later_ref, low_ref, unit_ref, left_ref, next_ref = refs
    else:
        low_ref, unit_ref = refs
    low_ref[0:size, 0:size] = low_real
    low_ref[0:size, size:] = low_imag
    low_ref[size:, 0:size] = -low_imag
    low_ref[size:, size:] = low_real
    unit_ref[0] = unit_real
    unit_ref[1] = unit_imag
    if rotates:
        rho_real, rho_imag = rho_ref[0], rho_ref[1]
        left_real = dot_high(unit_real, rho_real) - dot_high(unit_imag, rho_imag)
        left_imag = dot_high(unit_real, rho_imag) + dot_high(unit_imag, rho_real)
        left_ref[0] = left_real
        left_ref[1] = left_imag
        real_diagonal = jnp.sum(left_real * unit_real + left_imag * unit_imag, axis=1, keepdims=True)
        row = jnp.sum(jnp.where(eye, real_diagonal + later_ref[0], 0.0), axis=0, keepdims=True)
        spread_rows(next_ref, row)


IN_VMEM = pl.BlockSpec(memory_space=pltpu.VMEM)
IN_HBM = pl.BlockSpec(memory_space=pl.ANY)


def call(body, outs, args, cost_estimate, scratch=(), scalars=0, streamed=(), streamed_outs=(), grant=8):
    specs = [pl.BlockSpec(memory_space=pltpu.SMEM)] * scalars
    specs += [IN_HBM if i in streamed else IN_VMEM for i in range(scalars, len(args))]
    return pl.pallas_call(
        body,
        out_shape=[
            pltpu.HBM(shape, kind) if i in streamed_outs else jax.ShapeDtypeStruct(shape, kind)
            for i, (shape, kind) in enumerate(outs)
        ],
        in_specs=specs,
        out_specs=[IN_HBM if i in streamed_outs else IN_VMEM for i in range(len(outs))],
        scratch_shapes=list(scratch),
        cost_estimate=cost_estimate,
        compiler_params=pltpu.CompilerParams(vmem_limit_bytes=grant * 2**20 if grant else None),
    )(*args)


def stream(outside, inside, semaphores, base, group, width, inward):
    lanes = lanes_of(base, 0, width)
    ends = (outside.at[:, lanes], inside.at[:, lanes])
    source, target = ends if inward else ends[::-1]
    return pltpu.make_async_copy(source, target, semaphores.at[group])


def solve(levels, hamiltonian, rho=None, later=None):
    size = hamiltonian.shape[0]
    outs = [((2 * size, 2 * size), jnp.bfloat16), ((2, size, size), jnp.float32)]
    args = (levels, hamiltonian)
    if rho is not None:
        outs += [((2, size, size), jnp.float32), (levels.shape, jnp.float32)]
        args += (rho, later)
    estimate = pl.CostEstimate(flops=4_000_000_000, bytes_accessed=1_000_000, transcendentals=0)
    return call(functools.partial(solve_kernel, rho is not None), outs, args, estimate)


def lanes_of(base, first, span):
    return pl.ds(pl.multiple_of(base + first, 128), span)


def sigma_into(sig_ref, row_ref, col_ref, base, rows, span):
    size = sig_ref.shape[0] // 2
    for start in range(0, size, rows):
        for first in range(0, sig_ref.shape[1], span):
            real, imag = pl.ds(start, rows), pl.ds(size + start, rows)
            lanes, here = lanes_of(base, first, span), pl.ds(first, span)
            green_real = row_ref[real, lanes].astype(jnp.float32)
            green_imag = row_ref[imag, lanes].astype(jnp.float32)
            other_real = col_ref[real, lanes].astype(jnp.float32)
            other_imag = col_ref[imag, lanes].astype(jnp.float32)
            square_real = (coupling * coupling) * (green_real * green_real - green_imag * green_imag)
            square_imag = (coupling * coupling * 2.0) * green_real * green_imag
            sig_ref[real, here] = (square_real * other_real - square_imag * other_imag).astype(jnp.bfloat16)
            sig_ref[imag, here] = (square_real * other_imag + square_imag * other_real).astype(jnp.bfloat16)


def overlap(sig, col):
    return lax.dot_general(sig, col, (((1,), (1,)), ((), ())), preferred_element_type=jnp.float32)


def advance_into(out_ref, low, source_ref, base, width, local=False):
    span = min(SPAN, width)
    for first in range(0, width, span):
        lanes = lanes_of(base, first, span)
        target = pl.ds(first, span) if local else lanes
        moved = jnp.dot(low, source_ref[:, lanes], preferred_element_type=jnp.float32)
        out_ref[:, target] = moved.astype(out_ref.dtype)


def row_form(low):
    size = low.shape[0] // 2
    top = jnp.concatenate([low[:size, :size], low[size:, :size]], axis=1)
    bottom = jnp.concatenate([low[:size, size:], low[:size, :size]], axis=1)
    return jnp.concatenate([top, bottom], axis=0)


def each_group(total_width, width, body):
    def step(g, carry):
        body(pl.multiple_of(g * width, width), g)
        return carry

    lax.fori_loop(0, total_width // width, step, 0)


def complex_sum(four):
    size = four.shape[0] // 2
    return four[:size, :size] - four[size:, size:], four[:size, size:] + four[size:, :size]


def finish_sum(acc, before_ref, base_ref, out_ref, scale):
    real, imag = complex_sum(scale * (acc[...] - before_ref[...]))
    if base_ref is not None:
        real, imag = base_ref[0] + real, base_ref[1] + imag
    out_ref[0] = real
    out_ref[1] = imag
    return real


def now_kernel(parts, last, me_ref, row_hbm, *refs):
    pieces, refs = refs[:parts], refs[parts:]
    if last:
        before_ref, known_ref, col_hbm, rho_out, level_out, acc, *refs = refs
    else:
        col_hbm, acc, *refs = refs
    sig, place, col_out, row_ref, held, sent, row_came, came = refs
    _, _, _, block, times = held.shape
    total_width, width = col_out.shape[1], sig.shape[1]
    group = width // times
    size = sig.shape[0] // 2
    direct = place.dtype == col_out.dtype
    arrivals = [pltpu.make_async_copy(pieces[r], held.at[r], came.at[r]) for r in range(parts)]
    for copy in arrivals:
        copy.start()
    each_group(total_width, width, lambda base, g: stream(row_hbm, row_ref, row_came, base, g, width, True).start())
    acc[...] = jnp.zeros_like(acc)
    for copy in arrivals:
        copy.wait()

    def body(base, g):
        first = lax.div(base, times)
        for r in range(parts):
            source = lax.bitwise_xor(me_ref[0], r) * block
            for part in range(2):
                rows = pl.ds(pl.multiple_of(part * size + source, block), block)
                for k in range(group):
                    value = held[r, part, first + k]
                    if direct:
                        col_out[rows, lanes_of(base, k * times, times)] = value
                    else:
                        place[rows, pl.ds(k * times, times)] = value.astype(place.dtype)
        if not direct:
            col_out[:, lanes_of(base, 0, width)] = place[...].astype(col_out.dtype)
        stream(col_hbm, col_out, sent, base, g, width, False).start()
        stream(row_hbm, row_ref, row_came, base, g, width, True).wait()
        sigma_into(sig, row_ref, col_out, base, 16, min(SPAN, width))
        acc[...] += overlap(sig[...], col_out[:, lanes_of(base, 0, width)])

    each_group(total_width, width, body)
    if last:
        real = finish_sum(acc, before_ref, known_ref, rho_out, step_length)
        spread_rows(level_out, diagonal_row(real))
    each_group(total_width, width, lambda base, g: stream(col_hbm, col_out, sent, base, g, width, False).wait())


def later_kernel(last, row_hbm, col_hbm, low_ref, *refs):
    if last:
        before_ref, row_to, col_to, sum_out, acc, *refs = refs
    else:
        row_to, col_to, acc, *refs = refs
    sig, row_ref, col_ref, row_out, col_out, row_came, col_came, row_went, col_went = refs
    total_width, width = row_ref.shape[1], sig.shape[1]

    def loads(base, g):
        return (
            stream(row_hbm, row_ref, row_came, base, g, width, True),
            stream(col_hbm, col_ref, col_came, base, g, width, True),
        )

    def stores(base, g):
        return (
            stream(row_to, row_out, row_went, base, g, width, False),
            stream(col_to, col_out, col_went, base, g, width, False),
        )

    def start(base, g):
        for copy in loads(base, g):
            copy.start()

    def wait(base, g):
        for copy in stores(base, g):
            copy.wait()

    each_group(total_width, width, start)
    acc[...] = jnp.zeros_like(acc)

    def body(base, g):
        for copy in loads(base, g):
            copy.wait()
        advance_into(row_out, row_form(low_ref[...]), row_ref, base, width)
        advance_into(col_out, low_ref[...], col_ref, base, width)
        for copy in stores(base, g):
            copy.start()
        sigma_into(sig, row_out, col_out, base, 16, min(SPAN, width))
        acc[...] += overlap(sig[...], col_out[:, lanes_of(base, 0, width)])

    each_group(total_width, width, body)
    if last:
        finish_sum(acc, before_ref, None, sum_out, step_length)
    each_group(total_width, width, wait)


def finish_kernel(left_ref, unit_ref, later_ref, unit_last_ref, last_ref, rho_ref):
    def right(real, imag, unit):
        turned_real, turned_imag = unit[0].T, unit[1].T
        return (
            dot_high(real, turned_real) + dot_high(imag, turned_imag),
            dot_high(imag, turned_real) - dot_high(real, turned_imag),
        )

    real, imag = right(left_ref[0], left_ref[1], unit_ref)
    real, imag = real + later_ref[0], imag + later_ref[1]
    unit_real, unit_imag = unit_last_ref[0], unit_last_ref[1]
    left_real = dot_high(unit_real, real) - dot_high(unit_imag, imag)
    left_imag = dot_high(unit_real, imag) + dot_high(unit_imag, real)
    real, imag = right(left_real, left_imag, unit_last_ref)
    rho_ref[0] = real + last_ref[0]
    rho_ref[1] = imag + last_ref[1]


def row_kernel(width, row_ref, low_ref, row_out):
    low = row_form(low_ref[...])
    each_group(row_ref.shape[1], width, lambda base, g: advance_into(row_out, low, row_ref, base, width))


def last_kernel(parts, me_ref, col_ref, low_first_ref, low_ref, low_last_ref, *refs):
    pieces, outs, (place, once, moved) = refs[:parts], refs[parts : 2 * parts], refs[2 * parts :]
    _, mirrored, block, times = pieces[0].shape
    size, width = moved.shape[0] // 2, moved.shape[1]
    count = col_ref.shape[1] // times

    def advance(out_ref, low, source_ref, base):
        span = min(SPAN, width)
        for first in range(0, width, span):
            source = source_ref[:, lanes_of(base, first, span)].astype(jnp.bfloat16)
            after = jnp.dot(low[...], source, preferred_element_type=jnp.float32)
            out_ref[:, pl.ds(first, span)] = after.astype(jnp.bfloat16).astype(out_ref.dtype)

    def cut(r, to):
        target = lax.bitwise_xor(me_ref[0], r) * block
        for part in range(2):
            rows = pl.ds(pl.multiple_of(part * size + target, block), block)
            for k in range(mirrored):
                outs[r][part, to + k] = moved[rows, pl.ds(k * times, times)].astype(outs[r].dtype)

    def body(base, g):
        first = lax.div(base, times)
        advance(once, low_ref, col_ref, base)
        advance(moved, low_last_ref, once, 0)
        for r in range(parts // 2):
            cut(r, first)

        @pl.when(first >= mirrored)
        def _():
            for r in range(parts // 2, parts):
                cut(r, first - mirrored)

    each_group(count * times, width, body)
    for r in range(parts):
        source = lax.bitwise_xor(me_ref[0], r) * block
        for part in range(2):
            rows = pl.ds(pl.multiple_of(part * size + source, block), block)
            for k in range(mirrored):
                place[rows, pl.ds(k * times, times)] = pieces[r][part, k].astype(place.dtype)
    advance(once, low_first_ref, place, 0)
    advance(place, low_ref, once, 0)
    advance(moved, low_last_ref, place, 0)
    for r in range(parts // 2):
        cut(r, count)


def cost(arrays, products):
    return pl.CostEstimate(flops=products * 2 * 256 * 256 * 4096, bytes_accessed=arrays * 2**21, transcendentals=0)


def place_type(block):
    return jnp.bfloat16 if block % 16 == 0 else jnp.float32


def sum_scratch(size, width):
    return [pltpu.VMEM((2 * size, 2 * size), jnp.float32), pltpu.VMEM((2 * size, width), jnp.bfloat16)]


def now_step(me, row, pieces, before=None, known=None, devices=0):
    parts = len(pieces)
    _, count, block, times = pieces[0].shape
    size = parts * block
    width = min(GROUP, count) * times
    groups = row.shape[1] // width
    square, history = ((2 * size, 2 * size), jnp.float32), (row.shape, jnp.bfloat16)
    args = (me, row, *pieces)
    scratch = sum_scratch(size, width)
    scratch += [pltpu.VMEM((2 * size, width), place_type(block))] + [pltpu.VMEM(row.shape, jnp.bfloat16)] * 2
    scratch += [pltpu.VMEM((parts,) + pieces[0].shape, jnp.bfloat16)]
    scratch += [pltpu.SemaphoreType.DMA((groups,))] * 2 + [pltpu.SemaphoreType.DMA((parts,))]
    body = functools.partial(now_kernel, parts, before is not None)
    if before is None:
        outs, scratch = [history, square], scratch[1:]
    else:
        outs, args = [history, ((2, size, size), jnp.float32), ((devices, 1, size), jnp.float32)], args + (before, known)
    return call(body, outs, args, cost(4, 2), scratch, 1, range(1, parts + 2), (0,), None)


def later_step(row, col, low, width, before=None):
    double = row.shape[0]
    square, history = ((double, double), jnp.float32), (row.shape, jnp.bfloat16)
    body = functools.partial(later_kernel, before is not None)
    scratch = sum_scratch(double // 2, width) + [pltpu.VMEM(row.shape, jnp.bfloat16)] * 4
    scratch += [pltpu.SemaphoreType.DMA((row.shape[1] // width,))] * 4
    if before is None:
        outs, args, scratch = [history, history, square], (row, col, low), scratch[1:]
    else:
        outs, args = [history, history, ((2, double // 2, double // 2), jnp.float32)], (row, col, low, before)
    return call(body, outs, args, cost(4, 3), scratch, 0, (0, 1), (0, 1), None)


def row_step(row, low, width):
    body = functools.partial(row_kernel, width)
    return call(body, [(row.shape, jnp.bfloat16)], (row, low), cost(2, 1))[0]


def last_step(me, col, pieces, low_first, low, low_last):
    double, parts = col.shape[0], len(pieces)
    _, mirrored, block, times = pieces[0].shape
    count = col.shape[1] // times
    near = ((2, count + mirrored, block, times), jnp.bfloat16)
    far = ((2, count - mirrored, block, times), jnp.bfloat16)
    outs = [near] * (parts // 2) + [far] * (parts - parts // 2)
    kind = place_type(block)
    scratch = [pltpu.VMEM((double, mirrored * times), k) for k in (kind, jnp.bfloat16, kind)]
    body = functools.partial(last_kernel, parts)
    return call(body, outs, (me, col, low_first, low, low_last, *pieces), cost(3, 2), scratch, 1)


def tree_sum(values):
    while len(values) > 1:
        values = [values[i] + values[i + 1] for i in range(0, len(values), 2)]
    return values[0]


def swap(value, name, r):
    return lax.ppermute(value, name, [(j, j ^ r) for j in range(lax.axis_size(name))])


def part_total(values):
    count = lax.axis_size("hist")
    rows = values.reshape(count, -1, values.shape[-1])
    share = jnp.sum(lax.all_to_all(rows, "hist", 0, 0, tiled=True), axis=0)
    return share


def whole_total(share, shape):
    count = lax.axis_size("hist")
    moved = [share]
    for r in range(1, lax.axis_size("col")):
        moved.append(swap(share, "col", r))
    share = tree_sum(moved)
    return lax.all_to_all(jnp.broadcast_to(share, (count,) + share.shape), "hist", 0, 0, tiled=True).reshape(shape)


def finish_rotation(left, unit):
    high = functools.partial(jnp.dot, precision=HIGH)
    real = high(left[0], unit[0].T) + high(left[1], unit[1].T)
    imag = high(left[1], unit[0].T) - high(left[0], unit[1].T)
    return jnp.stack([real, imag])


def rotate(unit, rho):
    high = functools.partial(jnp.dot, precision=HIGH)
    real = high(unit[0], rho[0]) - high(unit[1], rho[1])
    imag = high(unit[0], rho[1]) + high(unit[1], rho[0])
    return finish_rotation((real, imag), unit)


def gather_pieces(col):
    me, parts = lax.axis_index("col"), lax.axis_size("col")
    count = col.shape[1] // parts
    pieces = []
    for r in range(parts):
        piece = lax.dynamic_slice_in_dim(col, (me ^ r) * count, count, axis=1)
        pieces.append(swap(piece, "col", r) if r else piece)
    return pieces


def mirror_slices(col, mirrored):
    me, parts = lax.axis_index("col"), lax.axis_size("col")
    count = col.shape[1] // parts
    starts = [(me ^ r ^ (parts // 2)) * count for r in range(parts)]
    return [lax.dynamic_slice_in_dim(col, start, mirrored, axis=1) for start in starts]


def mirror_pieces(slices):
    pieces = []
    for r, piece in enumerate(slices):
        pieces.append(swap(piece, "col", r) if r else piece)
    return pieces


def return_pieces(pieces):
    me, parts = lax.axis_index("col"), lax.axis_size("col")
    _, near, block, times = pieces[0].shape
    mirrored = (near - pieces[-1].shape[1]) // 2
    count = near - mirrored
    out = jnp.zeros((2, parts * count, block, times), pieces[0].dtype)
    half = parts // 2
    for r in [half, 0] + [r for r in range(1, parts) if r != half]:
        moved = pieces[r] if r == 0 else swap(pieces[r], "col", r)
        if r < half:
            out = lax.dynamic_update_slice_in_dim(out, moved[:, :count], (me ^ r) * count, axis=1)
            out = lax.dynamic_update_slice_in_dim(out, moved[:, count:], (me ^ r ^ half) * count, axis=1)
        else:
            out = lax.dynamic_update_slice_in_dim(out, moved, (me ^ r) * count + mirrored, axis=1)
    return out


def per_device(less_row, less_col, great_row, great_col, density, hamiltonian):
    size, count, times = less_row.shape[1:]
    parts = lax.axis_size("col")
    devices = parts * lax.axis_size("hist")
    me = lax.axis_index("col").astype(jnp.int32).reshape(1)
    width = min(GROUP, count) * times
    mirrored = count // 4

    great_pieces = gather_pieces(great_col)
    less_pieces = gather_pieces(less_col)
    far_slices = (mirror_slices(great_col, mirrored), mirror_slices(less_col, mirrored))

    symmetric = 0.5 * (hamiltonian + hamiltonian.T)
    low_first, unit = solve(diagonal_row(density[0]).reshape(1, 1, size), symmetric)
    known = rotate(unit, density * (1.0 / devices))

    less = less_row.reshape(2 * size, count * times)
    great = great_row.reshape(2 * size, count * times)
    cols_great, minus = now_step(me, less, great_pieces)
    less, cols_great, minus_later = later_step(less, cols_great, low_first, width)
    less_pieces, far_slices, minus_later = lax.optimization_barrier((less_pieces, far_slices, minus_later))
    cols_less, rho, part = now_step(me, great, less_pieces, minus, known, devices)

    levels = lax.all_to_all(part, ("hist", "col"), 0, 0, tiled=True)
    great, cols_less, later = later_step(great, cols_less, low_first, width, minus_later)
    low, unit, left, part = solve(levels, symmetric, rho, later)

    levels = lax.all_to_all(part, ("hist", "col"), 0, 0, tiled=True)
    far_slices, _ = lax.optimization_barrier((far_slices, part))
    great_far = mirror_pieces(far_slices[0])
    less_far = mirror_pieces(far_slices[1])
    low_last, unit_last = solve(levels, symmetric)

    great_out = return_pieces(last_step(me, cols_great, great_far, low_first, low, low_last))
    less_out = last_step(me, cols_less, less_far, low_first, low, low_last)
    less_out = return_pieces(less_out)
    less, _, minus = later_step(less, cols_great, low, width)
    great, _, last = later_step(great, cols_less, low, width, minus)
    args = (left, unit, later, unit_last, last)
    estimate = pl.CostEstimate(flops=500_000_000, bytes_accessed=1_000_000, transcendentals=0)
    rho = call(finish_kernel, [(density.shape, jnp.float32)], args, estimate)[0]
    rho = whole_total(part_total(rho), density.shape)
    less_row_out = row_step(less, low_last, width).reshape(less_row.shape)
    great_row_out = row_step(great, low_last, width).reshape(great_row.shape)
    return (less_row_out, less_out, great_row_out, great_out, rho)


def solution(mesh):
    history = P(None, None, "col", "hist")
    return jax.shard_map(
        per_device,
        mesh=mesh,
        in_specs=(history, history, history, history, P(), P()),
        out_specs=(history, history, history, history, P()),
        check_vma=False,
    )
```

profile of v0, /device:TPU:0, one launch (start us, length us, event | category | flops | bytes accessed | tf_op | source)
XLA Modules:
  0.0 279.9 jit_solution(11163780012892175275)
XLA Ops:
  0.7 3.1 %constant_dynamic-slice_fusion.12 = (bf16[2,32,32,128]{3,2,1,0:T(8,128)(2,1)}, bf16[2,32,32,128]{3,2,1,0:T(8,128)(2,1)}, bf16[2,32,32,128]{3,2,1,0:T(8,128)(2,1)}, bf16[2,32,32,128]{3,2,1,0:T(8,128)(2,1)}) fusion(bf16[2,128,32,128]{3,2,1,0:T(8,128)(2,1)} %param.9, s32[]{:T(128)S(6)} %select_n.25, s32[]{:T(128)S(6)} %select_n.24, s32[]{:T(128)S(6)} %select_n.23, ...), kind=kLoop, calls=%fused_computation.62 | loop fusion | bytes 4194320 | tf_op jit(solution)/shard_map/dynamic_slice | solution.py:481
  3.8 3.1 %collective-permute-start = (bf16[2,32,32,128]{3,2,1,0:T(8,128)(2,1)}, bf16[2,32,32,128]{3,2,1,0:T(8,128)(2,1)}, u32[]{:S(2)}, u32[]{:S(2)}) collective-permute-start(bf16[2,32,32,128]{3,2,1,0:T(8,128)(2,1)} %get-tuple-element.123), channel_id=1, source_target_pairs={{0,1},{1,0},{2,3},{3,2},{4,5},{5,4},{6,7},{7,6},{8,9},{9,8},{10,11... | collective-permute-start | bytes 1572872 | tf_op jit(solution)/shard_map/ppermute | solution.py:443
  6.8 2.6 collective-permute-start.1
  9.4 1.5 constant_dynamic-slice_fusion.8
  11.8 3.5 %collective-permute-start.4 = (bf16[2,32,32,128]{3,2,1,0:T(8,128)(2,1)}, bf16[2,32,32,128]{3,2,1,0:T(8,128)(2,1)}, u32[]{:S(2)}, u32[]{:S(2)}) collective-permute-start(bf16[2,32,32,128]{3,2,1,0:T(8,128)(2,1)} %get-tuple-element.118), channel_id=1, source_target_pairs={{0,2},{1,3},{2,0},{3,1},{4,6},{5,7},{6,4},{7,5},{8,10},{9,11},{10,... | collective-permute-start | bytes 1572872 | tf_op jit(solution)/shard_map/ppermute | solution.py:443
  15.5 4.4 %shard_map.102 = (bf16[256,256]{1,0:T(8,128)(2,1)S(1)}, f32[2,128,128]{2,1,0:T(8,128)S(1)}) custom-call(f32[1,1,128]{2,1,0:T(1,128)S(1)} %bitcast.64, f32[128,128]{1,0:T(8,128)S(1)} %fusion.14.ham_ref), custom_call_target="tpu_custom_call" | custom-call | flops 4000000000 | bytes 1000000 | tf_op jit(solution)/shard_map/pallas_call | solution.py:117
  22.2 8.3 %collective-permute-done.refs_1_ = bf16[2,32,32,128]{3,2,1,0:T(8,128)(2,1)} collective-permute-done((bf16[2,32,32,128]{3,2,1,0:T(8,128)(2,1)}, bf16[2,32,32,128]{3,2,1,0:T(8,128)(2,1)}, u32[]{:S(2)}, u32[]{:S(2)}) %collective-permute-start) | collective-permute-done | bytes 524320 | tf_op jit(solution)/shard_map/ppermute | solution.py:443
  30.4 4.5 %collective-permute-start.5 = (bf16[2,32,32,128]{3,2,1,0:T(8,128)(2,1)}, bf16[2,32,32,128]{3,2,1,0:T(8,128)(2,1)}, u32[]{:S(2)}, u32[]{:S(2)}) collective-permute-start(bf16[2,32,32,128]{3,2,1,0:T(8,128)(2,1)} %get-tuple-element.117), channel_id=1, source_target_pairs={{0,3},{1,2},{2,1},{3,0},{4,7},{5,6},{6,5},{7,4},{8,11},{9,10},{10,... | collective-permute-start | bytes 1572872 | tf_op jit(solution)/shard_map/ppermute | solution.py:443
  35.3 4.0 %copy.19 = bf16[32,8,32,128]{3,1,2,0:T(8,128)(2,1)} copy(bf16[32,8,32,128]{3,2,1,0:T(8,128)(2,1)} %bitcast.69) | data formatting | bytes 4194304
  39.3 2.3 copy.18
  42.3 2.0 constant_dynamic-slice_fusion
  45.4 5.1 %shard_map.101 = (bf16[256,4096]{1,0:T(8,128)(2,1)}, f32[256,256]{1,0:T(8,128)}) custom-call(s32[1]{0:T(128)} %bitcast.me_ref, bf16[256,4096]{1,0:T(8,128)(2,1)} %bitcast.67, bf16[2,32,32,128]{3,2,1,0:T(8,128)(2,1)} %get-tuple-element.124.refs_0_, bf16[2,32,32,128]{3,2,1,0:T(8,128)(2,1)} %collective-permute-done.refs_1_, ...), custom_call_target="tpu_custom_call" | custom-call | flops 1073741824 | bytes 8388608 | tf_op jit(solution)/shard_map/pallas_call | solution.py:117
  50.5 7.6 %shard_map.103 = (bf16[256,4096]{1,0:T(8,128)(2,1)}, bf16[256,4096]{1,0:T(8,128)(2,1)}, f32[256,256]{1,0:T(8,128)}) custom-call(bf16[256,4096]{1,0:T(8,128)(2,1)} %bitcast.68, bf16[256,4096]{1,0:T(8,128)(2,1)} %get-tuple-element.57.col_hbm, bf16[256,256]{1,0:T(8,128)(2,1)} %copy-done.18), custom_call_target="tpu_custom_call" | custom-call | flops 1610612736 | bytes 8388608 | tf_op jit(solution)/shard_map/pallas_call | solution.py:117
  58.2 32.1 %collective-permute-done.4.refs_2_ = bf16[2,32,32,128]{3,2,1,0:T(8,128)(2,1)} collective-permute-done((bf16[2,32,32,128]{3,2,1,0:T(8,128)(2,1)}, bf16[2,32,32,128]{3,2,1,0:T(8,128)(2,1)}, u32[]{:S(2)}, u32[]{:S(2)}) %collective-permute-start.4) | collective-permute-done | bytes 524320 | tf_op jit(solution)/shard_map/ppermute | solution.py:443
  90.3 6.2 %shard_map.104 = (bf16[256,4096]{1,0:T(8,128)(2,1)}, f32[2,128,128]{2,1,0:T(8,128)}, f32[32,1,128]{2,1,0:T(1,128)}) custom-call(s32[1]{0:T(128)} %bitcast.me_ref, bf16[256,4096]{1,0:T(8,128)(2,1)} %bitcast.65, bf16[2,32,32,128]{3,2,1,0:T(8,128)(2,1)} %get-tuple-element.62.refs_0_, bf16[2,32,32,128]{3,2,1,0:T(8,128)(2,1)} %copy-done.31, ...), custom_call_target="tpu_custom_call" | custom-call | flops 1073741824 | bytes 8388608 | tf_op jit(solution)/shard_map/pallas_call | solution.py:117
  96.5 13.9 %all-to-all-start = ((f32[32,1,128]{2,1,0:T(1,128)}), f32[32,1,128]{2,1,0:T(1,128)S(1)}, u32[]{:S(2)}, u32[]{:S(2)}) async-start(f32[32,1,128]{2,1,0:T(1,128)} %get-tuple-element.68), calls=%async_computation | async-start | bytes 32768 | tf_op jit(solution)/shard_map/all_to_all | solution.py:540
  110.4 7.8 %shard_map.105 = (bf16[256,4096]{1,0:T(8,128)(2,1)}, bf16[256,4096]{1,0:T(8,128)(2,1)}, f32[2,128,128]{2,1,0:T(8,128)}) custom-call(bf16[256,4096]{1,0:T(8,128)(2,1)} %bitcast.66, bf16[256,4096]{1,0:T(8,128)(2,1)} %get-tuple-element.70.col_hbm, bf16[256,256]{1,0:T(8,128)(2,1)} %copy-done.18, f32[256,256]{1,0:T(8,128)} %get-tuple-element.71.refs_0_), custom_call_target="tpu_custom_call" | custom-call | flops 1610612736 | bytes 8388608 | tf_op jit(solution)/shard_map/pallas_call | solution.py:117
  119.1 5.4 %shard_map.106 = (bf16[256,256]{1,0:T(8,128)(2,1)S(1)}, f32[2,128,128]{2,1,0:T(8,128)S(1)}, f32[2,128,128]{2,1,0:T(8,128)S(1)}, f32[32,1,128]{2,1,0:T(1,128)}) custom-call(f32[32,1,128]{2,1,0:T(1,128)S(1)} %all-to-all-done.levels_ref, f32[128,128]{1,0:T(8,128)S(1)} %fusion.14.ham_ref, f32[2,128,128]{2,1,0:T(8,128)S(1)} %copy-done.15, ...), custom_call_target="tpu_custom_call" | custom-call | flops 4000000000 | bytes 1000000 | tf_op jit(solution)/shard_map/pallas_call | solution.py:117
  125.2 5.7 %all-to-all-start.1 = ((f32[32,1,128]{2,1,0:T(1,128)}), f32[32,1,128]{2,1,0:T(1,128)S(1)}, u32[]{:S(2)}, u32[]{:S(2)}) async-start(f32[32,1,128]{2,1,0:T(1,128)} %get-tuple-element.75), calls=%async_computation.1 | async-start | bytes 32768 | tf_op jit(solution)/shard_map/all_to_all | solution.py:544
  130.8 1.8 collective-permute-start.12
  132.7 2.4 collective-permute-start.13
  135.3 7.7 %shard_map.107 = (bf16[256,4096]{1,0:T(8,128)(2,1)}, bf16[256,4096]{1,0:T(8,128)(2,1)}, f32[256,256]{1,0:T(8,128)}) custom-call(bf16[256,4096]{1,0:T(8,128)(2,1)} %get-tuple-element.59.row_hbm, bf16[256,4096]{1,0:T(8,128)(2,1)} %get-tuple-element.60.col_hbm.col_ref, bf16[256,256]{1,0:T(8,128)(2,1)} %copy-done.21), custom_call_target="tpu_custom_call" | custom-call | flops 1610612736 | bytes 8388608 | tf_op jit(solution)/shard_map/pallas_call | solution.py:117
  143.0 7.7 %shard_map.111 = (bf16[256,4096]{1,0:T(8,128)(2,1)}, bf16[256,4096]{1,0:T(8,128)(2,1)}, f32[2,128,128]{2,1,0:T(8,128)}) custom-call(bf16[256,4096]{1,0:T(8,128)(2,1)} %get-tuple-element.94.row_hbm, bf16[256,4096]{1,0:T(8,128)(2,1)} %get-tuple-element.77.col_ref.col_hbm, bf16[256,256]{1,0:T(8,128)(2,1)} %copy-done.21, f32[256,256]{1,0:T(8,128)} %get-tuple-element.95.refs_0_), custom_call_target="tpu_custom_call" | custom-call | flops 1610612736 | bytes 8388608 | tf_op jit(solution)/shard_map/pallas_call | solution.py:117
  150.7 4.4 %shard_map.108 = (bf16[256,256]{1,0:T(8,128)(2,1)S(1)}, f32[2,128,128]{2,1,0:T(8,128)S(1)}) custom-call(f32[32,1,128]{2,1,0:T(1,128)S(1)} %all-to-all-done.1.levels_ref, f32[128,128]{1,0:T(8,128)S(1)} %fusion.14.ham_ref), custom_call_target="tpu_custom_call" | custom-call | flops 4000000000 | bytes 1000000 | tf_op jit(solution)/shard_map/pallas_call | solution.py:117
  155.2 2.2 shard_map.114
  157.4 3.9 %all-to-all-start.2 = ((f32[8,32,128]{2,1,0:T(8,128)}), f32[8,32,128]{2,1,0:T(8,128)S(1)}, u32[]{:S(2)}, u32[]{:S(2)}) async-start(f32[8,32,128]{2,1,0:T(8,128)} %bitcast.10), calls=%async_computation.2 | async-start | bytes 262144 | tf_op jit(solution)/shard_map/all_to_all | solution.py:449
  162.0 1.6 copy-done.17
  163.6 3.8 %shard_map.113 = (bf16[2,40,32,128]{3,2,1,0:T(8,128)(2,1)S(1)}, bf16[2,40,32,128]{3,2,1,0:T(8,128)(2,1)S(1)}, bf16[2,24,32,128]{3,2,1,0:T(8,128)(2,1)}, bf16[2,24,32,128]{3,2,1,0:T(8,128)(2,1)S(1)}) custom-call(s32[1]{0:T(128)} %bitcast.me_ref, bf16[256,4096]{1,0:T(8,128)(2,1)S(1)} %copy-done.17, bf16[256,256]{1,0:T(8,128)(2,1)S(1)} %copy-done.19, ...), custom_call_target="tpu_custom_call" | custom-call | flops 1073741824 | bytes 6291456 | tf_op jit(solution)/shard_map/pallas_call | solution.py:117
  168.2 3.4 %collective-permute-start.15 = (bf16[2,24,32,128]{3,2,1,0:T(8,128)(2,1)}, bf16[2,24,32,128]{3,2,1,0:T(8,128)(2,1)}, u32[]{:S(2)}, u32[]{:S(2)}) collective-permute-start(bf16[2,24,32,128]{3,2,1,0:T(8,128)(2,1)} %get-tuple-element.101), channel_id=1, source_target_pairs={{0,2},{1,3},{2,0},{3,1},{4,6},{5,7},{6,4},{7,5},{8,10},{9,11},{10,... | collective-permute-start | bytes 1179656 | tf_op jit(solution)/shard_map/ppermute | solution.py:443
  172.7 3.3 %collective-permute-start.20 = (f32[32,128]{1,0:T(8,128)S(1)}, f32[32,128]{1,0:T(8,128)S(1)}, u32[]{:S(2)}, u32[]{:S(2)}) collective-permute-start(f32[32,128]{1,0:T(8,128)S(1)} %reduce_sum.19), channel_id=1, source_target_pairs={{0,3},{1,2},{2,1},{3,0},{4,7},{5,6},{6,5},{7,4},{8,11},{9,10},{10,... | collective-permute-start | bytes 49160 | tf_op jit(solution)/shard_map/ppermute | solution.py:443
  176.0 1.6 copy-done.1
  177.6 1.3 shard_map.112
  179.0 2.3 collective-permute-done.18
  181.3 1.5 collective-permute-start.7
  182.8 11.1 %collective-permute-done.19 = f32[32,128]{1,0:T(8,128)S(1)} collective-permute-done((f32[32,128]{1,0:T(8,128)S(1)}, f32[32,128]{1,0:T(8,128)S(1)}, u32[]{:S(2)}, u32[]{:S(2)}) %collective-permute-start.19) | collective-permute-done | bytes 16416 | tf_op jit(solution)/shard_map/ppermute | solution.py:443
  193.9 2.6 collective-permute-start.8
  197.1 4.2 %all-to-all-start.3 = ((f32[8,32,128]{2,1,0:T(8,128)}), f32[8,32,128]{2,1,0:T(8,128)}, u32[]{:S(2)}, u32[]{:S(2)}) async-start(f32[8,32,128]{2,1,0:T(8,128)} %broadcast_in_dim.8), calls=%async_computation.3 | async-start | bytes 262144 | tf_op jit(solution)/shard_map/all_to_all | solution.py:459
  206.9 1.6 copy-done.16
  210.3 4.1 %shard_map.110 = (bf16[2,40,32,128]{3,2,1,0:T(8,128)(2,1)S(1)}, bf16[2,40,32,128]{3,2,1,0:T(8,128)(2,1)}, bf16[2,24,32,128]{3,2,1,0:T(8,128)(2,1)}, bf16[2,24,32,128]{3,2,1,0:T(8,128)(2,1)S(1)}) custom-call(s32[1]{0:T(128)} %bitcast.me_ref, bf16[256,4096]{1,0:T(8,128)(2,1)S(1)} %copy-done.16, bf16[256,256]{1,0:T(8,128)(2,1)S(1)} %copy-done.20, ...), custom_call_target="tpu_custom_call" | custom-call | flops 1073741824 | bytes 6291456 | tf_op jit(solution)/shard_map/pallas_call | solution.py:117
  215.6 1.3 shard_map.109
  217.0 1.8 copy.15
  218.8 1.8 copy.14
  221.2 2.6 collective-permute-start.17
  223.8 1.8 collective-permute-start.11
  227.0 7.8 %collective-permute-done.9 = bf16[2,24,32,128]{3,2,1,0:T(8,128)(2,1)} collective-permute-done((bf16[2,24,32,128]{3,2,1,0:T(8,128)(2,1)}, bf16[2,24,32,128]{3,2,1,0:T(8,128)(2,1)}, u32[]{:S(2)}, u32[]{:S(2)}) %collective-permute-start.9) | collective-permute-done | bytes 393248 | tf_op jit(solution)/shard_map/ppermute | solution.py:443
  236.3 18.7 %collective-permute-done.16 = bf16[2,40,32,128]{3,2,1,0:T(8,128)(2,1)} collective-permute-done((bf16[2,40,32,128]{3,2,1,0:T(8,128)(2,1)S(1)}, bf16[2,40,32,128]{3,2,1,0:T(8,128)(2,1)}, u32[]{:S(2)}, u32[]{:S(2)}) %collective-permute-start.16) | collective-permute-done | bytes 655392 | tf_op jit(solution)/shard_map/ppermute | solution.py:443
  256.2 19.6 %collective-permute-done.10 = bf16[2,40,32,128]{3,2,1,0:T(8,128)(2,1)S(1)} collective-permute-done((bf16[2,40,32,128]{3,2,1,0:T(8,128)(2,1)}, bf16[2,40,32,128]{3,2,1,0:T(8,128)(2,1)S(1)}, u32[]{:S(2)}, u32[]{:S(2)}) %collective-permute-start.10) | collective-permute-done | bytes 655392 | tf_op jit(solution)/shard_map/ppermute | solution.py:443
  278.0 1.9 copy.33
  (122 shorter events, 25.7 us)
Async XLA Ops:
  0.7 8.8 %copy-start.27 = (bf16[2,128,32,128]{3,2,1,0:T(8,128)(2,1)S(1)}, bf16[2,128,32,128]{3,2,1,0:T(8,128)(2,1)}, u32[]{:S(2)}) copy-start(bf16[2,128,32,128]{3,2,1,0:T(8,128)(2,1)} %param.7) | copy-start | bytes 6291460
  3.8 26.6 %collective-permute-start = (bf16[2,32,32,128]{3,2,1,0:T(8,128)(2,1)}, bf16[2,32,32,128]{3,2,1,0:T(8,128)(2,1)}, u32[]{:S(2)}, u32[]{:S(2)}) collective-permute-start(bf16[2,32,32,128]{3,2,1,0:T(8,128)(2,1)} %get-tuple-element.123), channel_id=1, source_target_pairs={{0,1},{1,0},{2,3},{3,2},{4,5},{5,4},{6,7},{7,6},{8,9},{9,8},{10,11... | collective-permute-start | bytes 1572872 | tf_op jit(solution)/shard_map/ppermute | solution.py:443
  6.8 38.5 %collective-permute-start.1 = (bf16[2,32,32,128]{3,2,1,0:T(8,128)(2,1)}, bf16[2,32,32,128]{3,2,1,0:T(8,128)(2,1)}, u32[]{:S(2)}, u32[]{:S(2)}) collective-permute-start(bf16[2,32,32,128]{3,2,1,0:T(8,128)(2,1)} %get-tuple-element.122), channel_id=1, source_target_pairs={{0,2},{1,3},{2,0},{3,1},{4,6},{5,7},{6,4},{7,5},{8,10},{9,11},{10,... | collective-permute-start | bytes 1572872 | tf_op jit(solution)/shard_map/ppermute | solution.py:443
  9.4 5.9 %copy-start.32 = (f32[2,128,128]{2,1,0:T(8,128)S(1)}, f32[2,128,128]{2,1,0:T(8,128)}, u32[]{:S(2)}) copy-start(f32[2,128,128]{2,1,0:T(8,128)} %param.10) | copy-start | bytes 393220
  9.4 5.9 %copy-start.33 = (f32[128,128]{1,0:T(8,128)S(1)}, f32[128,128]{1,0:T(8,128)}, u32[]{:S(2)}) copy-start(f32[128,128]{1,0:T(8,128)} %param.11) | copy-start | bytes 196612
  9.4 35.9 %collective-permute-start.2 = (bf16[2,32,32,128]{3,2,1,0:T(8,128)(2,1)}, bf16[2,32,32,128]{3,2,1,0:T(8,128)(2,1)}, u32[]{:S(2)}, u32[]{:S(2)}) collective-permute-start(bf16[2,32,32,128]{3,2,1,0:T(8,128)(2,1)} %get-tuple-element.121), channel_id=1, source_target_pairs={{0,3},{1,2},{2,1},{3,0},{4,7},{5,6},{6,5},{7,4},{8,11},{9,10},{10,... | collective-permute-start | bytes 1572872 | tf_op jit(solution)/shard_map/ppermute | solution.py:443
  10.9 47.2 %collective-permute-start.3 = (bf16[2,32,32,128]{3,2,1,0:T(8,128)(2,1)}, bf16[2,32,32,128]{3,2,1,0:T(8,128)(2,1)S(1)}, u32[]{:S(2)}, u32[]{:S(2)}) collective-permute-start(bf16[2,32,32,128]{3,2,1,0:T(8,128)(2,1)} %get-tuple-element.119), channel_id=1, source_target_pairs={{0,1},{1,0},{2,3},{3,2},{4,5},{5,4},{6,7},{7,6},{8,9},{9,8},{10,11... | collective-permute-start | bytes 1572872 | tf_op jit(solution)/shard_map/ppermute | solution.py:443
  11.8 78.5 %collective-permute-start.4 = (bf16[2,32,32,128]{3,2,1,0:T(8,128)(2,1)}, bf16[2,32,32,128]{3,2,1,0:T(8,128)(2,1)}, u32[]{:S(2)}, u32[]{:S(2)}) collective-permute-start(bf16[2,32,32,128]{3,2,1,0:T(8,128)(2,1)} %get-tuple-element.118), channel_id=1, source_target_pairs={{0,2},{1,3},{2,0},{3,1},{4,6},{5,7},{6,4},{7,5},{8,10},{9,11},{10,... | collective-permute-start | bytes 1572872 | tf_op jit(solution)/shard_map/ppermute | solution.py:443
  30.4 59.9 %collective-permute-start.5 = (bf16[2,32,32,128]{3,2,1,0:T(8,128)(2,1)}, bf16[2,32,32,128]{3,2,1,0:T(8,128)(2,1)}, u32[]{:S(2)}, u32[]{:S(2)}) collective-permute-start(bf16[2,32,32,128]{3,2,1,0:T(8,128)(2,1)} %get-tuple-element.117), channel_id=1, source_target_pairs={{0,3},{1,2},{2,1},{3,0},{4,7},{5,6},{6,5},{7,4},{8,11},{9,10},{10,... | collective-permute-start | bytes 1572872 | tf_op jit(solution)/shard_map/ppermute | solution.py:443
  35.2 4.1 %copy-start.30 = (bf16[2,128,32,128]{3,2,1,0:T(8,128)(2,1)S(1)}, bf16[2,128,32,128]{3,2,1,0:T(8,128)(2,1)}, u32[]{:S(2)}) copy-start(bf16[2,128,32,128]{3,2,1,0:T(8,128)(2,1)} %param.8) | copy-start | bytes 6291460
  58.1 32.2 %copy-start.31 = (bf16[2,32,32,128]{3,2,1,0:T(8,128)(2,1)}, bf16[2,32,32,128]{3,2,1,0:T(8,128)(2,1)S(1)}, u32[]{:S(2)}) copy-start(bf16[2,32,32,128]{3,2,1,0:T(8,128)(2,1)S(1)} %collective-permute-done.3.refs_1_) | copy-start | bytes 1572868
  96.5 21.7 %all-to-all-start = ((f32[32,1,128]{2,1,0:T(1,128)}), f32[32,1,128]{2,1,0:T(1,128)S(1)}, u32[]{:S(2)}, u32[]{:S(2)}) async-start(f32[32,1,128]{2,1,0:T(1,128)} %get-tuple-element.68), calls=%async_computation | async-start | bytes 32768 | tf_op jit(solution)/shard_map/all_to_all | solution.py:540
  110.4 7.8 %copy-start.15 = (f32[2,128,128]{2,1,0:T(8,128)S(1)}, f32[2,128,128]{2,1,0:T(8,128)}, u32[]{:S(2)}) copy-start(f32[2,128,128]{2,1,0:T(8,128)} %get-tuple-element.69.refs_0_) | copy-start | bytes 393220
  118.2 0.9 copy-start.24
  125.2 25.6 %all-to-all-start.1 = ((f32[32,1,128]{2,1,0:T(1,128)}), f32[32,1,128]{2,1,0:T(1,128)S(1)}, u32[]{:S(2)}, u32[]{:S(2)}) async-start(f32[32,1,128]{2,1,0:T(1,128)} %get-tuple-element.75), calls=%async_computation.1 | async-start | bytes 32768 | tf_op jit(solution)/shard_map/all_to_all | solution.py:544
  130.8 31.1 %collective-permute-start.12 = (bf16[2,8,32,128]{3,2,1,0:T(8,128)(2,1)S(1)}, bf16[2,8,32,128]{3,2,1,0:T(8,128)(2,1)S(1)}, u32[]{:S(2)}, u32[]{:S(2)}) collective-permute-start(bf16[2,8,32,128]{3,2,1,0:T(8,128)(2,1)S(1)} %get-tuple-element.98), channel_id=1, source_target_pairs={{0,1},{1,0},{2,3},{3,2},{4,5},{5,4},{6,7},{7,6},{8,9},{9,8},{10,11... | collective-permute-start | bytes 393224 | tf_op jit(solution)/shard_map/ppermute | solution.py:443
  132.7 29.3 %collective-permute-start.13 = (bf16[2,8,32,128]{3,2,1,0:T(8,128)(2,1)S(1)}, bf16[2,8,32,128]{3,2,1,0:T(8,128)(2,1)S(1)}, u32[]{:S(2)}, u32[]{:S(2)}) collective-permute-start(bf16[2,8,32,128]{3,2,1,0:T(8,128)(2,1)S(1)} %get-tuple-element.99), channel_id=1, source_target_pairs={{0,2},{1,3},{2,0},{3,1},{4,6},{5,7},{6,4},{7,5},{8,10},{9,11},{10,... | collective-permute-start | bytes 393224 | tf_op jit(solution)/shard_map/ppermute | solution.py:443
  135.1 26.9 %collective-permute-start.14 = (bf16[2,8,32,128]{3,2,1,0:T(8,128)(2,1)S(1)}, bf16[2,8,32,128]{3,2,1,0:T(8,128)(2,1)S(1)}, u32[]{:S(2)}, u32[]{:S(2)}) collective-permute-start(bf16[2,8,32,128]{3,2,1,0:T(8,128)(2,1)S(1)} %get-tuple-element.100), channel_id=1, source_target_pairs={{0,3},{1,2},{2,1},{3,0},{4,7},{5,6},{6,5},{7,4},{8,11},{9,10},{10,... | collective-permute-start | bytes 393224 | tf_op jit(solution)/shard_map/ppermute | solution.py:443
  150.7 4.5 %copy-start.25 = (f32[2,128,128]{2,1,0:T(8,128)S(1)}, f32[2,128,128]{2,1,0:T(8,128)}, u32[]{:S(2)}) copy-start(f32[2,128,128]{2,1,0:T(8,128)} %get-tuple-element.72.refs_1_.later_ref) | copy-start | bytes 393220
  150.7 4.5 %copy-start.26 = (f32[2,128,128]{2,1,0:T(8,128)S(1)}, f32[2,128,128]{2,1,0:T(8,128)}, u32[]{:S(2)}) copy-start(f32[2,128,128]{2,1,0:T(8,128)} %get-tuple-element.108.last_ref) | copy-start | bytes 393220
  155.1 6.8 %copy-start.19 = (bf16[256,256]{1,0:T(8,128)(2,1)S(1)}, bf16[256,256]{1,0:T(8,128)(2,1)}, u32[]{:S(2)}) copy-start(bf16[256,256]{1,0:T(8,128)(2,1)} %copy-done.18) | copy-start | bytes 393220
  155.2 6.8 %copy-start.22 = (bf16[256,256]{1,0:T(8,128)(2,1)S(1)}, bf16[256,256]{1,0:T(8,128)(2,1)}, u32[]{:S(2)}) copy-start(bf16[256,256]{1,0:T(8,128)(2,1)} %copy-done.21) | copy-start | bytes 393220
  157.4 14.1 %all-to-all-start.2 = ((f32[8,32,128]{2,1,0:T(8,128)}), f32[8,32,128]{2,1,0:T(8,128)S(1)}, u32[]{:S(2)}, u32[]{:S(2)}) async-start(f32[8,32,128]{2,1,0:T(8,128)} %bitcast.10), calls=%async_computation.2 | async-start | bytes 262144 | tf_op jit(solution)/shard_map/all_to_all | solution.py:449
  161.4 39.9 %collective-permute-start.6 = (bf16[2,8,32,128]{3,2,1,0:T(8,128)(2,1)}, bf16[2,8,32,128]{3,2,1,0:T(8,128)(2,1)S(1)}, u32[]{:S(2)}, u32[]{:S(2)}) collective-permute-start(bf16[2,8,32,128]{3,2,1,0:T(8,128)(2,1)} %get-tuple-element.87), channel_id=1, source_target_pairs={{0,1},{1,0},{2,3},{3,2},{4,5},{5,4},{6,7},{7,6},{8,9},{9,8},{10,11... | collective-permute-start | bytes 393224 | tf_op jit(solution)/shard_map/ppermute | solution.py:443
  162.0 1.6 copy-start.17
  168.2 10.7 %copy-start.5 = (bf16[2,24,32,128]{3,2,1,0:T(8,128)(2,1)}, bf16[2,24,32,128]{3,2,1,0:T(8,128)(2,1)S(1)}, u32[]{:S(2)}) copy-start(bf16[2,24,32,128]{3,2,1,0:T(8,128)(2,1)S(1)} %get-tuple-element.104) | copy-start | bytes 1179652
  168.2 55.6 %collective-permute-start.15 = (bf16[2,24,32,128]{3,2,1,0:T(8,128)(2,1)}, bf16[2,24,32,128]{3,2,1,0:T(8,128)(2,1)}, u32[]{:S(2)}, u32[]{:S(2)}) collective-permute-start(bf16[2,24,32,128]{3,2,1,0:T(8,128)(2,1)} %get-tuple-element.101), channel_id=1, source_target_pairs={{0,2},{1,3},{2,0},{3,1},{4,6},{5,7},{6,4},{7,5},{8,10},{9,11},{10,... | collective-permute-start | bytes 1179656 | tf_op jit(solution)/shard_map/ppermute | solution.py:443
  171.6 9.7 %collective-permute-start.18 = (f32[32,128]{1,0:T(8,128)S(1)}, f32[32,128]{1,0:T(8,128)S(1)}, u32[]{:S(2)}, u32[]{:S(2)}) collective-permute-start(f32[32,128]{1,0:T(8,128)S(1)} %reduce_sum.19), channel_id=1, source_target_pairs={{0,1},{1,0},{2,3},{3,2},{4,5},{5,4},{6,7},{7,6},{8,9},{9,8},{10,11... | collective-permute-start | bytes 49160 | tf_op jit(solution)/shard_map/ppermute | solution.py:443
  171.7 22.2 %collective-permute-start.19 = (f32[32,128]{1,0:T(8,128)S(1)}, f32[32,128]{1,0:T(8,128)S(1)}, u32[]{:S(2)}, u32[]{:S(2)}) collective-permute-start(f32[32,128]{1,0:T(8,128)S(1)} %reduce_sum.19), channel_id=1, source_target_pairs={{0,2},{1,3},{2,0},{3,1},{4,6},{5,7},{6,4},{7,5},{8,10},{9,11},{10,... | collective-permute-start | bytes 49160 | tf_op jit(solution)/shard_map/ppermute | solution.py:443
  172.7 23.7 %collective-permute-start.20 = (f32[32,128]{1,0:T(8,128)S(1)}, f32[32,128]{1,0:T(8,128)S(1)}, u32[]{:S(2)}, u32[]{:S(2)}) collective-permute-start(f32[32,128]{1,0:T(8,128)S(1)} %reduce_sum.19), channel_id=1, source_target_pairs={{0,3},{1,2},{2,1},{3,0},{4,7},{5,6},{6,5},{7,4},{8,11},{9,10},{10,... | collective-permute-start | bytes 49160 | tf_op jit(solution)/shard_map/ppermute | solution.py:443
  176.0 1.6 copy-start.1
  181.3 20.7 %collective-permute-start.7 = (bf16[2,8,32,128]{3,2,1,0:T(8,128)(2,1)}, bf16[2,8,32,128]{3,2,1,0:T(8,128)(2,1)S(1)}, u32[]{:S(2)}, u32[]{:S(2)}) collective-permute-start(bf16[2,8,32,128]{3,2,1,0:T(8,128)(2,1)} %get-tuple-element.88), channel_id=1, source_target_pairs={{0,2},{1,3},{2,0},{3,1},{4,6},{5,7},{6,4},{7,5},{8,10},{9,11},{10,... | collective-permute-start | bytes 393224 | tf_op jit(solution)/shard_map/ppermute | solution.py:443
  193.9 8.8 %collective-permute-start.8 = (bf16[2,8,32,128]{3,2,1,0:T(8,128)(2,1)}, bf16[2,8,32,128]{3,2,1,0:T(8,128)(2,1)S(1)}, u32[]{:S(2)}, u32[]{:S(2)}) collective-permute-start(bf16[2,8,32,128]{3,2,1,0:T(8,128)(2,1)} %get-tuple-element.89), channel_id=1, source_target_pairs={{0,3},{1,2},{2,1},{3,0},{4,7},{5,6},{6,5},{7,4},{8,11},{9,10},{10,... | collective-permute-start | bytes 393224 | tf_op jit(solution)/shard_map/ppermute | solution.py:443
  197.1 26.7 %all-to-all-start.3 = ((f32[8,32,128]{2,1,0:T(8,128)}), f32[8,32,128]{2,1,0:T(8,128)}, u32[]{:S(2)}, u32[]{:S(2)}) async-start(f32[8,32,128]{2,1,0:T(8,128)} %broadcast_in_dim.8), calls=%async_computation.3 | async-start | bytes 262144 | tf_op jit(solution)/shard_map/all_to_all | solution.py:459
  201.3 14.3 %copy-start = (bf16[256,4096]{1,0:T(8,128)(2,1)S(1)}, bf16[256,4096]{1,0:T(8,128)(2,1)}, u32[]{:S(2)}) copy-start(bf16[256,4096]{1,0:T(8,128)(2,1)} %get-tuple-element.74.row_ref) | copy-start | bytes 6291460
  203.3 0.9 copy-start.2
  206.9 1.6 copy-start.16
  214.4 2.5 copy-start.7
  214.5 20.4 %collective-permute-start.9 = (bf16[2,24,32,128]{3,2,1,0:T(8,128)(2,1)}, bf16[2,24,32,128]{3,2,1,0:T(8,128)(2,1)}, u32[]{:S(2)}, u32[]{:S(2)}) collective-permute-start(bf16[2,24,32,128]{3,2,1,0:T(8,128)(2,1)} %get-tuple-element.90), channel_id=1, source_target_pairs={{0,2},{1,3},{2,0},{3,1},{4,6},{5,7},{6,4},{7,5},{8,10},{9,11},{10,... | collective-permute-start | bytes 1179656 | tf_op jit(solution)/shard_map/ppermute | solution.py:443
  218.8 1.8 copy-start.4
  218.8 2.5 copy-start.6
  218.8 5.0 %copy-start.8 = (bf16[2,24,32,128]{3,2,1,0:T(8,128)(2,1)S(1)}, bf16[2,24,32,128]{3,2,1,0:T(8,128)(2,1)}, u32[]{:S(2)}) copy-start(bf16[2,24,32,128]{3,2,1,0:T(8,128)(2,1)} %copy-done.7) | copy-start | bytes 1179652
  220.6 34.5 %collective-permute-start.16 = (bf16[2,40,32,128]{3,2,1,0:T(8,128)(2,1)S(1)}, bf16[2,40,32,128]{3,2,1,0:T(8,128)(2,1)}, u32[]{:S(2)}, u32[]{:S(2)}) collective-permute-start(bf16[2,40,32,128]{3,2,1,0:T(8,128)(2,1)S(1)} %copy-done.4), channel_id=1, source_target_pairs={{0,1},{1,0},{2,3},{3,2},{4,5},{5,4},{6,7},{7,6},{8,9},{9,8},{10,11... | collective-permute-start | bytes 1966088 | tf_op jit(solution)/shard_map/ppermute | solution.py:443
  221.2 55.6 %collective-permute-start.17 = (bf16[2,24,32,128]{3,2,1,0:T(8,128)(2,1)S(1)}, bf16[2,24,32,128]{3,2,1,0:T(8,128)(2,1)}, u32[]{:S(2)}, u32[]{:S(2)}) collective-permute-start(bf16[2,24,32,128]{3,2,1,0:T(8,128)(2,1)S(1)} %copy-done.6), channel_id=1, source_target_pairs={{0,3},{1,2},{2,1},{3,0},{4,7},{5,6},{6,5},{7,4},{8,11},{9,10},{10,... | collective-permute-start | bytes 1179656 | tf_op jit(solution)/shard_map/ppermute | solution.py:443
  223.8 52.0 %collective-permute-start.10 = (bf16[2,40,32,128]{3,2,1,0:T(8,128)(2,1)}, bf16[2,40,32,128]{3,2,1,0:T(8,128)(2,1)S(1)}, u32[]{:S(2)}, u32[]{:S(2)}) collective-permute-start(bf16[2,40,32,128]{3,2,1,0:T(8,128)(2,1)} %get-tuple-element.92), channel_id=1, source_target_pairs={{0,1},{1,0},{2,3},{3,2},{4,5},{5,4},{6,7},{7,6},{8,9},{9,8},{10,11... | collective-permute-start | bytes 1966088 | tf_op jit(solution)/shard_map/ppermute | solution.py:443
  223.8 54.1 %collective-permute-start.11 = (bf16[2,24,32,128]{3,2,1,0:T(8,128)(2,1)S(1)}, bf16[2,24,32,128]{3,2,1,0:T(8,128)(2,1)S(1)}, u32[]{:S(2)}, u32[]{:S(2)}) collective-permute-start(bf16[2,24,32,128]{3,2,1,0:T(8,128)(2,1)S(1)} %copy-done.8), channel_id=1, source_target_pairs={{0,3},{1,2},{2,1},{3,0},{4,7},{5,6},{6,5},{7,4},{8,11},{9,10},{10,... | collective-permute-start | bytes 1179656 | tf_op jit(solution)/shard_map/ppermute | solution.py:443
  277.9 2.0 copy-start.29
  278.0 1.9 copy-start.28
  (11 other events, 8.6 us)
where the time goes:
time: 281 us; the launch traced here: 280 us
  waiting for transfers between devices  101 us (36%)
  Pallas kernels  69.1 us (25%)
  starting transfers between devices  65.3 us (23%)
  local copies, waits for them, and re-layouts  40.6 us (14%)
    ppermute x21, waiting for transfers between devices, swap(): lax.ppermute(value, name, [(j, j ^ r) for j in range(lax.axis_size(name))])  101 us
    pallas_call x14, Pallas kernels, call(): pl.pallas_call(body, out_shape=[pltpu.HBM(shape, kind) if i in streamed_o...  69.1 us
    ppermute x21, starting transfers between devices, swap(): lax.ppermute(value, name, [(j, j ^ r) for j in range(lax.axis_size(name))])  37.6 us
    unnamed x74, local copies, waits for them, and re-layouts  27.3 us
    all_to_all x2, starting transfers between devices, per_device(): levels = lax.all_to_all(part, ('hist', 'col'), 0, 0, tiled=True)  19.5 us
  transfers between devices with their start and end apart: 25, of which 8 were waited for; matrix products, arithmetic and copies ran while one was open for 8% of the time, Pallas kernels for 21%

commit v1 on v0

--- a/solution.py
+++ b/solution.py
@@ -524,7 +524,8 @@
 
     great_pieces = gather_pieces(great_col)
     less_pieces = gather_pieces(less_col)
-    far_slices = (mirror_slices(great_col, mirrored), mirror_slices(less_col, mirrored))
+    great_slices = mirror_slices(great_col, mirrored)
+    less_slices = mirror_slices(less_col, mirrored)
 
     symmetric = 0.5 * (hamiltonian + hamiltonian.T)
     low_first, unit = solve(diagonal_row(density[0]).reshape(1, 1, size), symmetric)
@@ -534,17 +535,18 @@
     great = great_row.reshape(2 * size, count * times)
     cols_great, minus = now_step(me, less, great_pieces)
     less, cols_great, minus_later = later_step(less, cols_great, low_first, width)
-    less_pieces, far_slices, minus_later = lax.optimization_barrier((less_pieces, far_slices, minus_later))
+    less_pieces, minus_later = lax.optimization_barrier((less_pieces, minus_later))
     cols_less, rho, part = now_step(me, great, less_pieces, minus, known, devices)
 
     levels = lax.all_to_all(part, ("hist", "col"), 0, 0, tiled=True)
+    great_slices, _ = lax.optimization_barrier((great_slices, part))
+    great_far = mirror_pieces(great_slices)
     great, cols_less, later = later_step(great, cols_less, low_first, width, minus_later)
     low, unit, left, part = solve(levels, symmetric, rho, later)
 
     levels = lax.all_to_all(part, ("hist", "col"), 0, 0, tiled=True)
-    far_slices, _ = lax.optimization_barrier((far_slices, part))
-    great_far = mirror_pieces(far_slices[0])
-    less_far = mirror_pieces(far_slices[1])
+    less_slices, _ = lax.optimization_barrier((less_slices, part))
+    less_far = mirror_pieces(less_slices)
     low_last, unit_last = solve(levels, symmetric)
 
     great_out = return_pieces(last_step(me, cols_great, great_far, low_first, low, low_last))

time: 281 us -> 271 us (0.964)
  local copies, waits for them, and re-layouts: 40.6 us -> 35.1 us
  waiting for transfers between devices: 101 us -> 97.2 us
    unnamed x74 -> x58, local copies, waits for them, and re-layouts: 27.3 us -> 18.8 us
    ppermute x21, waiting for transfers between devices: 101 us -> 97.2 us  [swap(): lax.ppermute(value, name, [(j, j ^ r) for j in range(lax.axis_size(name))])]
  transfers between devices with their start and end apart: 25 -> 25, of which waited for: 8 -> 7; matrix products, arithmetic and copies ran while one was open for 8% -> 9% of each run, Pallas kernels for 21% -> 24%
where the time goes in v1:
time: 271 us
  waiting for transfers between devices  97.2 us (36%)
  Pallas kernels  69.8 us (26%)
  starting transfers between devices  64.6 us (24%)
  local copies, waits for them, and re-layouts  35.1 us (13%)
    ppermute x21, waiting for transfers between devices, swap(): lax.ppermute(value, name, [(j, j ^ r) for j in range(lax.axis_size(name))])  97.2 us
    pallas_call x14, Pallas kernels, call(): pl.pallas_call(body, out_shape=[pltpu.HBM(shape, kind) if i in streamed_o...  69.8 us
    ppermute x21, starting transfers between devices, swap(): lax.ppermute(value, name, [(j, j ^ r) for j in range(lax.axis_size(name))])  37.6 us
    all_to_all x2, starting transfers between devices, per_device(): levels = lax.all_to_all(part, ('hist', 'col'), 0, 0, tiled=True)  18.8 us
    unnamed x58, local copies, waits for them, and re-layouts  18.8 us
  transfers between devices with their start and end apart: 25, of which 7 were waited for; matrix products, arithmetic and copies ran while one was open for 9% of the time, Pallas kernels for 24%

profile of v1, /device:TPU:0, one launch (start us, length us, event | category | flops | bytes accessed | tf_op | source)
XLA Modules:
  0.0 270.6 jit_solution(3225611463907278855)
XLA Ops:
  0.7 3.1 %constant_dynamic-slice_fusion.12 = (bf16[2,32,32,128]{3,2,1,0:T(8,128)(2,1)}, bf16[2,32,32,128]{3,2,1,0:T(8,128)(2,1)}, bf16[2,32,32,128]{3,2,1,0:T(8,128)(2,1)}, bf16[2,32,32,128]{3,2,1,0:T(8,128)(2,1)}) fusion(bf16[2,128,32,128]{3,2,1,0:T(8,128)(2,1)} %param.9, s32[]{:T(128)S(6)} %select_n.25, s32[]{:T(128)S(6)} %select_n.24, s32[]{:T(128)S(6)} %select_n.23, ...), kind=kLoop, calls=%fused_computation.62 | loop fusion | bytes 4194320 | tf_op jit(solution)/shard_map/dynamic_slice | solution.py:481
  3.8 3.1 %collective-permute-start = (bf16[2,32,32,128]{3,2,1,0:T(8,128)(2,1)}, bf16[2,32,32,128]{3,2,1,0:T(8,128)(2,1)}, u32[]{:S(2)}, u32[]{:S(2)}) collective-permute-start(bf16[2,32,32,128]{3,2,1,0:T(8,128)(2,1)} %get-tuple-element.107), channel_id=1, source_target_pairs={{0,1},{1,0},{2,3},{3,2},{4,5},{5,4},{6,7},{7,6},{8,9},{9,8},{10,11... | collective-permute-start | bytes 1572872 | tf_op jit(solution)/shard_map/ppermute | solution.py:443
  6.8 2.6 collective-permute-start.1
  9.4 1.5 constant_dynamic-slice_fusion.8
  11.8 3.5 %collective-permute-start.4 = (bf16[2,32,32,128]{3,2,1,0:T(8,128)(2,1)}, bf16[2,32,32,128]{3,2,1,0:T(8,128)(2,1)S(1)}, u32[]{:S(2)}, u32[]{:S(2)}) collective-permute-start(bf16[2,32,32,128]{3,2,1,0:T(8,128)(2,1)} %get-tuple-element.102), channel_id=1, source_target_pairs={{0,2},{1,3},{2,0},{3,1},{4,6},{5,7},{6,4},{7,5},{8,10},{9,11},{10,... | collective-permute-start | bytes 1572872 | tf_op jit(solution)/shard_map/ppermute | solution.py:443
  15.5 4.4 %shard_map.102 = (bf16[256,256]{1,0:T(8,128)(2,1)S(1)}, f32[2,128,128]{2,1,0:T(8,128)S(1)}) custom-call(f32[1,1,128]{2,1,0:T(1,128)S(1)} %bitcast.64, f32[128,128]{1,0:T(8,128)S(1)} %fusion.14.ham_ref), custom_call_target="tpu_custom_call" | custom-call | flops 4000000000 | bytes 1000000 | tf_op jit(solution)/shard_map/pallas_call | solution.py:117
  22.1 8.3 %collective-permute-done.refs_1_ = bf16[2,32,32,128]{3,2,1,0:T(8,128)(2,1)} collective-permute-done((bf16[2,32,32,128]{3,2,1,0:T(8,128)(2,1)}, bf16[2,32,32,128]{3,2,1,0:T(8,128)(2,1)}, u32[]{:S(2)}, u32[]{:S(2)}) %collective-permute-start) | collective-permute-done | bytes 524320 | tf_op jit(solution)/shard_map/ppermute | solution.py:443
  30.4 4.5 %collective-permute-start.5 = (bf16[2,32,32,128]{3,2,1,0:T(8,128)(2,1)}, bf16[2,32,32,128]{3,2,1,0:T(8,128)(2,1)}, u32[]{:S(2)}, u32[]{:S(2)}) collective-permute-start(bf16[2,32,32,128]{3,2,1,0:T(8,128)(2,1)} %get-tuple-element.101), channel_id=1, source_target_pairs={{0,3},{1,2},{2,1},{3,0},{4,7},{5,6},{6,5},{7,4},{8,11},{9,10},{10,... | collective-permute-start | bytes 1572872 | tf_op jit(solution)/shard_map/ppermute | solution.py:443
  35.3 2.3 copy.19
  37.6 2.3 copy.18
  41.7 3.6 %collective-permute-done.1.refs_2_ = bf16[2,32,32,128]{3,2,1,0:T(8,128)(2,1)} collective-permute-done((bf16[2,32,32,128]{3,2,1,0:T(8,128)(2,1)}, bf16[2,32,32,128]{3,2,1,0:T(8,128)(2,1)}, u32[]{:S(2)}, u32[]{:S(2)}) %collective-permute-start.1) | collective-permute-done | bytes 524320 | tf_op jit(solution)/shard_map/ppermute | solution.py:443
  45.4 5.1 %shard_map.101 = (bf16[256,4096]{1,0:T(8,128)(2,1)}, f32[256,256]{1,0:T(8,128)}) custom-call(s32[1]{0:T(128)} %bitcast.me_ref, bf16[256,4096]{1,0:T(8,128)(2,1)} %bitcast.67, bf16[2,32,32,128]{3,2,1,0:T(8,128)(2,1)} %get-tuple-element.108.refs_0_, bf16[2,32,32,128]{3,2,1,0:T(8,128)(2,1)} %collective-permute-done.refs_1_, ...), custom_call_target="tpu_custom_call" | custom-call | flops 1073741824 | bytes 8388608 | tf_op jit(solution)/shard_map/pallas_call | solution.py:117
  50.5 7.7 %shard_map.103 = (bf16[256,4096]{1,0:T(8,128)(2,1)}, bf16[256,4096]{1,0:T(8,128)(2,1)}, f32[256,256]{1,0:T(8,128)}) custom-call(bf16[256,4096]{1,0:T(8,128)(2,1)} %bitcast.68, bf16[256,4096]{1,0:T(8,128)(2,1)} %get-tuple-element.49.col_hbm, bf16[256,256]{1,0:T(8,128)(2,1)} %copy-done.8), custom_call_target="tpu_custom_call" | custom-call | flops 1610612736 | bytes 8388608 | tf_op jit(solution)/shard_map/pallas_call | solution.py:117
  58.2 32.0 %collective-permute-done.4.refs_2_ = bf16[2,32,32,128]{3,2,1,0:T(8,128)(2,1)S(1)} collective-permute-done((bf16[2,32,32,128]{3,2,1,0:T(8,128)(2,1)}, bf16[2,32,32,128]{3,2,1,0:T(8,128)(2,1)S(1)}, u32[]{:S(2)}, u32[]{:S(2)}) %collective-permute-start.4) | collective-permute-done | bytes 524320 | tf_op jit(solution)/shard_map/ppermute | solution.py:443
  91.0 6.1 %shard_map.104 = (bf16[256,4096]{1,0:T(8,128)(2,1)}, f32[2,128,128]{2,1,0:T(8,128)}, f32[32,1,128]{2,1,0:T(1,128)}) custom-call(s32[1]{0:T(128)} %bitcast.me_ref, bf16[256,4096]{1,0:T(8,128)(2,1)} %bitcast.65, bf16[2,32,32,128]{3,2,1,0:T(8,128)(2,1)} %get-tuple-element.54.refs_0_, bf16[2,32,32,128]{3,2,1,0:T(8,128)(2,1)} %copy-done.22, ...), custom_call_target="tpu_custom_call" | custom-call | flops 1073741824 | bytes 8388608 | tf_op jit(solution)/shard_map/pallas_call | solution.py:117
  97.1 13.2 %all-to-all-start = ((f32[32,1,128]{2,1,0:T(1,128)}), f32[32,1,128]{2,1,0:T(1,128)S(1)}, u32[]{:S(2)}, u32[]{:S(2)}) async-start(f32[32,1,128]{2,1,0:T(1,128)} %get-tuple-element.60), calls=%async_computation | async-start | bytes 32768 | tf_op jit(solution)/shard_map/all_to_all | solution.py:541
  110.3 1.7 collective-permute-start.12
  111.9 2.4 collective-permute-start.13
  114.7 7.8 %shard_map.105 = (bf16[256,4096]{1,0:T(8,128)(2,1)}, bf16[256,4096]{1,0:T(8,128)(2,1)}, f32[2,128,128]{2,1,0:T(8,128)}) custom-call(bf16[256,4096]{1,0:T(8,128)(2,1)} %bitcast.66, bf16[256,4096]{1,0:T(8,128)(2,1)} %get-tuple-element.62.col_hbm, bf16[256,256]{1,0:T(8,128)(2,1)} %copy-done.8, f32[256,256]{1,0:T(8,128)} %get-tuple-element.63.refs_0_), custom_call_target="tpu_custom_call" | custom-call | flops 1610612736 | bytes 8388608 | tf_op jit(solution)/shard_map/pallas_call | solution.py:117
  123.4 5.4 %shard_map.106 = (bf16[256,256]{1,0:T(8,128)(2,1)S(1)}, f32[2,128,128]{2,1,0:T(8,128)S(1)}, f32[2,128,128]{2,1,0:T(8,128)S(1)}, f32[32,1,128]{2,1,0:T(1,128)}) custom-call(f32[32,1,128]{2,1,0:T(1,128)S(1)} %all-to-all-done.levels_ref, f32[128,128]{1,0:T(8,128)S(1)} %fusion.14.ham_ref, f32[2,128,128]{2,1,0:T(8,128)S(1)} %copy-done.5, ...), custom_call_target="tpu_custom_call" | custom-call | flops 4000000000 | bytes 1000000 | tf_op jit(solution)/shard_map/pallas_call | solution.py:117
  129.6 5.7 %all-to-all-start.1 = ((f32[32,1,128]{2,1,0:T(1,128)}), f32[32,1,128]{2,1,0:T(1,128)S(1)}, u32[]{:S(2)}, u32[]{:S(2)}) async-start(f32[32,1,128]{2,1,0:T(1,128)} %get-tuple-element.67), calls=%async_computation.1 | async-start | bytes 32768 | tf_op jit(solution)/shard_map/all_to_all | solution.py:547
  135.2 7.7 %shard_map.107 = (bf16[256,4096]{1,0:T(8,128)(2,1)}, bf16[256,4096]{1,0:T(8,128)(2,1)}, f32[256,256]{1,0:T(8,128)}) custom-call(bf16[256,4096]{1,0:T(8,128)(2,1)} %get-tuple-element.51.row_hbm, bf16[256,4096]{1,0:T(8,128)(2,1)} %get-tuple-element.52.col_hbm.col_ref, bf16[256,256]{1,0:T(8,128)(2,1)} %copy-done.11), custom_call_target="tpu_custom_call" | custom-call | flops 1610612736 | bytes 8388608 | tf_op jit(solution)/shard_map/pallas_call | solution.py:117
  142.9 7.8 %shard_map.111 = (bf16[256,4096]{1,0:T(8,128)(2,1)}, bf16[256,4096]{1,0:T(8,128)(2,1)}, f32[2,128,128]{2,1,0:T(8,128)}) custom-call(bf16[256,4096]{1,0:T(8,128)(2,1)} %get-tuple-element.78.row_hbm, bf16[256,4096]{1,0:T(8,128)(2,1)} %get-tuple-element.69.col_ref.col_hbm, bf16[256,256]{1,0:T(8,128)(2,1)} %copy-done.11, f32[256,256]{1,0:T(8,128)} %get-tuple-element.79.refs_0_), custom_call_target="tpu_custom_call" | custom-call | flops 1610612736 | bytes 8388608 | tf_op jit(solution)/shard_map/pallas_call | solution.py:117
  150.7 4.4 %shard_map.108 = (bf16[256,256]{1,0:T(8,128)(2,1)S(1)}, f32[2,128,128]{2,1,0:T(8,128)S(1)}) custom-call(f32[32,1,128]{2,1,0:T(1,128)S(1)} %all-to-all-done.1.levels_ref, f32[128,128]{1,0:T(8,128)S(1)} %fusion.14.ham_ref), custom_call_target="tpu_custom_call" | custom-call | flops 4000000000 | bytes 1000000 | tf_op jit(solution)/shard_map/pallas_call | solution.py:117
  155.2 2.2 shard_map.114
  157.5 3.9 %all-to-all-start.2 = ((f32[8,32,128]{2,1,0:T(8,128)}), f32[8,32,128]{2,1,0:T(8,128)S(1)}, u32[]{:S(2)}, u32[]{:S(2)}) async-start(f32[8,32,128]{2,1,0:T(8,128)} %bitcast.10), calls=%async_computation.2 | async-start | bytes 262144 | tf_op jit(solution)/shard_map/all_to_all | solution.py:449
  161.4 1.9 constant_dynamic-slice_fusion.4
  163.3 1.5 collective-permute-start.6
  164.8 1.6 copy-done.7
  166.4 3.8 %shard_map.113 = (bf16[2,40,32,128]{3,2,1,0:T(8,128)(2,1)S(1)}, bf16[2,40,32,128]{3,2,1,0:T(8,128)(2,1)S(1)}, bf16[2,24,32,128]{3,2,1,0:T(8,128)(2,1)}, bf16[2,24,32,128]{3,2,1,0:T(8,128)(2,1)S(1)}) custom-call(s32[1]{0:T(128)} %bitcast.me_ref, bf16[256,4096]{1,0:T(8,128)(2,1)S(1)} %copy-done.7, bf16[256,256]{1,0:T(8,128)(2,1)S(1)} %copy-done.9, ...), custom_call_target="tpu_custom_call" | custom-call | flops 1073741824 | bytes 6291456 | tf_op jit(solution)/shard_map/pallas_call | solution.py:117
  171.0 2.5 collective-permute-start.15
  174.6 3.4 %collective-permute-start.20 = (f32[32,128]{1,0:T(8,128)S(1)}, f32[32,128]{1,0:T(8,128)S(1)}, u32[]{:S(2)}, u32[]{:S(2)}) collective-permute-start(f32[32,128]{1,0:T(8,128)S(1)} %reduce_sum.19), channel_id=1, source_target_pairs={{0,3},{1,2},{2,1},{3,0},{4,7},{5,6},{6,5},{7,4},{8,11},{9,10},{10,... | collective-permute-start | bytes 49160 | tf_op jit(solution)/shard_map/ppermute | solution.py:443
  178.0 1.6 copy-done.1
  179.6 1.3 shard_map.112
  180.9 2.3 collective-permute-done.18
  183.2 1.5 collective-permute-start.7
  184.7 11.0 %collective-permute-done.19 = f32[32,128]{1,0:T(8,128)S(1)} collective-permute-done((f32[32,128]{1,0:T(8,128)S(1)}, f32[32,128]{1,0:T(8,128)S(1)}, u32[]{:S(2)}, u32[]{:S(2)}) %collective-permute-start.19) | collective-permute-done | bytes 16416 | tf_op jit(solution)/shard_map/ppermute | solution.py:443
  195.7 3.1 %collective-permute-start.8 = (bf16[2,8,32,128]{3,2,1,0:T(8,128)(2,1)}, bf16[2,8,32,128]{3,2,1,0:T(8,128)(2,1)}, u32[]{:S(2)}, u32[]{:S(2)}) collective-permute-start(bf16[2,8,32,128]{3,2,1,0:T(8,128)(2,1)} %get-tuple-element.73), channel_id=1, source_target_pairs={{0,3},{1,2},{2,1},{3,0},{4,7},{5,6},{6,5},{7,4},{8,11},{9,10},{10,... | collective-permute-start | bytes 393224 | tf_op jit(solution)/shard_map/ppermute | solution.py:443
  199.5 4.2 %all-to-all-start.3 = ((f32[8,32,128]{2,1,0:T(8,128)}), f32[8,32,128]{2,1,0:T(8,128)}, u32[]{:S(2)}, u32[]{:S(2)}) async-start(f32[8,32,128]{2,1,0:T(8,128)} %broadcast_in_dim.8), calls=%async_computation.3 | async-start | bytes 262144 | tf_op jit(solution)/shard_map/all_to_all | solution.py:459
  203.7 1.6 copy-done
  205.3 1.3 shard_map.109
  206.6 1.8 copy.15
  208.4 1.8 copy.14
  211.2 4.8 %shard_map.110 = (bf16[2,40,32,128]{3,2,1,0:T(8,128)(2,1)S(1)}, bf16[2,40,32,128]{3,2,1,0:T(8,128)(2,1)S(1)}, bf16[2,24,32,128]{3,2,1,0:T(8,128)(2,1)}, bf16[2,24,32,128]{3,2,1,0:T(8,128)(2,1)S(1)}) custom-call(s32[1]{0:T(128)} %bitcast.me_ref, bf16[256,4096]{1,0:T(8,128)(2,1)S(1)} %copy-done.6, bf16[256,256]{1,0:T(8,128)(2,1)S(1)} %copy-done.10, ...), custom_call_target="tpu_custom_call" | custom-call | flops 1073741824 | bytes 6291456 | tf_op jit(solution)/shard_map/pallas_call | solution.py:117
  215.9 2.6 collective-permute-start.9
  222.2 27.0 %collective-permute-done.9 = bf16[2,24,32,128]{3,2,1,0:T(8,128)(2,1)} collective-permute-done((bf16[2,24,32,128]{3,2,1,0:T(8,128)(2,1)}, bf16[2,24,32,128]{3,2,1,0:T(8,128)(2,1)}, u32[]{:S(2)}, u32[]{:S(2)}) %collective-permute-start.9) | collective-permute-done | bytes 393248 | tf_op jit(solution)/shard_map/ppermute | solution.py:443
  253.8 12.9 %collective-permute-done.10 = bf16[2,40,32,128]{3,2,1,0:T(8,128)(2,1)} collective-permute-done((bf16[2,40,32,128]{3,2,1,0:T(8,128)(2,1)S(1)}, bf16[2,40,32,128]{3,2,1,0:T(8,128)(2,1)}, u32[]{:S(2)}, u32[]{:S(2)}) %collective-permute-start.10) | collective-permute-done | bytes 655392 | tf_op jit(solution)/shard_map/ppermute | solution.py:443
  268.9 1.7 copy.33
  (107 shorter events, 22.0 us)
Async XLA Ops:
  0.7 8.8 %copy-start.17 = (bf16[2,128,32,128]{3,2,1,0:T(8,128)(2,1)S(1)}, bf16[2,128,32,128]{3,2,1,0:T(8,128)(2,1)}, u32[]{:S(2)}) copy-start(bf16[2,128,32,128]{3,2,1,0:T(8,128)(2,1)} %param.7) | copy-start | bytes 6291460
  3.8 26.6 %collective-permute-start = (bf16[2,32,32,128]{3,2,1,0:T(8,128)(2,1)}, bf16[2,32,32,128]{3,2,1,0:T(8,128)(2,1)}, u32[]{:S(2)}, u32[]{:S(2)}) collective-permute-start(bf16[2,32,32,128]{3,2,1,0:T(8,128)(2,1)} %get-tuple-element.107), channel_id=1, source_target_pairs={{0,1},{1,0},{2,3},{3,2},{4,5},{5,4},{6,7},{7,6},{8,9},{9,8},{10,11... | collective-permute-start | bytes 1572872 | tf_op jit(solution)/shard_map/ppermute | solution.py:443
  6.8 38.5 %collective-permute-start.1 = (bf16[2,32,32,128]{3,2,1,0:T(8,128)(2,1)}, bf16[2,32,32,128]{3,2,1,0:T(8,128)(2,1)}, u32[]{:S(2)}, u32[]{:S(2)}) collective-permute-start(bf16[2,32,32,128]{3,2,1,0:T(8,128)(2,1)} %get-tuple-element.106), channel_id=1, source_target_pairs={{0,2},{1,3},{2,0},{3,1},{4,6},{5,7},{6,4},{7,5},{8,10},{9,11},{10,... | collective-permute-start | bytes 1572872 | tf_op jit(solution)/shard_map/ppermute | solution.py:443
  9.4 5.8 %copy-start.24 = (f32[2,128,128]{2,1,0:T(8,128)S(1)}, f32[2,128,128]{2,1,0:T(8,128)}, u32[]{:S(2)}) copy-start(f32[2,128,128]{2,1,0:T(8,128)} %param.10) | copy-start | bytes 393220
  9.4 5.9 %copy-start.25 = (f32[128,128]{1,0:T(8,128)S(1)}, f32[128,128]{1,0:T(8,128)}, u32[]{:S(2)}) copy-start(f32[128,128]{1,0:T(8,128)} %param.11) | copy-start | bytes 196612
  9.4 35.9 %collective-permute-start.2 = (bf16[2,32,32,128]{3,2,1,0:T(8,128)(2,1)}, bf16[2,32,32,128]{3,2,1,0:T(8,128)(2,1)}, u32[]{:S(2)}, u32[]{:S(2)}) collective-permute-start(bf16[2,32,32,128]{3,2,1,0:T(8,128)(2,1)} %get-tuple-element.105), channel_id=1, source_target_pairs={{0,3},{1,2},{2,1},{3,0},{4,7},{5,6},{6,5},{7,4},{8,11},{9,10},{10,... | collective-permute-start | bytes 1572872 | tf_op jit(solution)/shard_map/ppermute | solution.py:443
  10.9 47.3 %collective-permute-start.3 = (bf16[2,32,32,128]{3,2,1,0:T(8,128)(2,1)}, bf16[2,32,32,128]{3,2,1,0:T(8,128)(2,1)S(1)}, u32[]{:S(2)}, u32[]{:S(2)}) collective-permute-start(bf16[2,32,32,128]{3,2,1,0:T(8,128)(2,1)} %get-tuple-element.103), channel_id=1, source_target_pairs={{0,1},{1,0},{2,3},{3,2},{4,5},{5,4},{6,7},{7,6},{8,9},{9,8},{10,11... | collective-permute-start | bytes 1572872 | tf_op jit(solution)/shard_map/ppermute | solution.py:443
  11.8 78.4 %collective-permute-start.4 = (bf16[2,32,32,128]{3,2,1,0:T(8,128)(2,1)}, bf16[2,32,32,128]{3,2,1,0:T(8,128)(2,1)S(1)}, u32[]{:S(2)}, u32[]{:S(2)}) collective-permute-start(bf16[2,32,32,128]{3,2,1,0:T(8,128)(2,1)} %get-tuple-element.102), channel_id=1, source_target_pairs={{0,2},{1,3},{2,0},{3,1},{4,6},{5,7},{6,4},{7,5},{8,10},{9,11},{10,... | collective-permute-start | bytes 1572872 | tf_op jit(solution)/shard_map/ppermute | solution.py:443
  15.4 19.8 %copy-start.20 = (bf16[2,128,32,128]{3,2,1,0:T(8,128)(2,1)S(1)}, bf16[2,128,32,128]{3,2,1,0:T(8,128)(2,1)}, u32[]{:S(2)}) copy-start(bf16[2,128,32,128]{3,2,1,0:T(8,128)(2,1)} %param.6) | copy-start | bytes 6291460
  30.4 59.8 %collective-permute-start.5 = (bf16[2,32,32,128]{3,2,1,0:T(8,128)(2,1)}, bf16[2,32,32,128]{3,2,1,0:T(8,128)(2,1)}, u32[]{:S(2)}, u32[]{:S(2)}) collective-permute-start(bf16[2,32,32,128]{3,2,1,0:T(8,128)(2,1)} %get-tuple-element.101), channel_id=1, source_target_pairs={{0,3},{1,2},{2,1},{3,0},{4,7},{5,6},{6,5},{7,4},{8,11},{9,10},{10,... | collective-permute-start | bytes 1572872 | tf_op jit(solution)/shard_map/ppermute | solution.py:443
  35.3 2.3 copy-start.21
  58.2 32.0 %copy-start.22 = (bf16[2,32,32,128]{3,2,1,0:T(8,128)(2,1)}, bf16[2,32,32,128]{3,2,1,0:T(8,128)(2,1)S(1)}, u32[]{:S(2)}) copy-start(bf16[2,32,32,128]{3,2,1,0:T(8,128)(2,1)S(1)} %collective-permute-done.3.refs_1_) | copy-start | bytes 1572868
  97.1 25.4 %all-to-all-start = ((f32[32,1,128]{2,1,0:T(1,128)}), f32[32,1,128]{2,1,0:T(1,128)S(1)}, u32[]{:S(2)}, u32[]{:S(2)}) async-start(f32[32,1,128]{2,1,0:T(1,128)} %get-tuple-element.60), calls=%async_computation | async-start | bytes 32768 | tf_op jit(solution)/shard_map/all_to_all | solution.py:541
  110.3 54.5 %collective-permute-start.12 = (bf16[2,8,32,128]{3,2,1,0:T(8,128)(2,1)S(1)}, bf16[2,8,32,128]{3,2,1,0:T(8,128)(2,1)S(1)}, u32[]{:S(2)}, u32[]{:S(2)}) collective-permute-start(bf16[2,8,32,128]{3,2,1,0:T(8,128)(2,1)S(1)} %get-tuple-element.82), channel_id=1, source_target_pairs={{0,1},{1,0},{2,3},{3,2},{4,5},{5,4},{6,7},{7,6},{8,9},{9,8},{10,11... | collective-permute-start | bytes 393224 | tf_op jit(solution)/shard_map/ppermute | solution.py:443
  111.9 52.8 %collective-permute-start.13 = (bf16[2,8,32,128]{3,2,1,0:T(8,128)(2,1)S(1)}, bf16[2,8,32,128]{3,2,1,0:T(8,128)(2,1)S(1)}, u32[]{:S(2)}, u32[]{:S(2)}) collective-permute-start(bf16[2,8,32,128]{3,2,1,0:T(8,128)(2,1)S(1)} %get-tuple-element.83), channel_id=1, source_target_pairs={{0,2},{1,3},{2,0},{3,1},{4,6},{5,7},{6,4},{7,5},{8,10},{9,11},{10,... | collective-permute-start | bytes 393224 | tf_op jit(solution)/shard_map/ppermute | solution.py:443
  114.4 50.4 %collective-permute-start.14 = (bf16[2,8,32,128]{3,2,1,0:T(8,128)(2,1)S(1)}, bf16[2,8,32,128]{3,2,1,0:T(8,128)(2,1)S(1)}, u32[]{:S(2)}, u32[]{:S(2)}) collective-permute-start(bf16[2,8,32,128]{3,2,1,0:T(8,128)(2,1)S(1)} %get-tuple-element.84), channel_id=1, source_target_pairs={{0,3},{1,2},{2,1},{3,0},{4,7},{5,6},{6,5},{7,4},{8,11},{9,10},{10,... | collective-permute-start | bytes 393224 | tf_op jit(solution)/shard_map/ppermute | solution.py:443
  114.7 7.8 %copy-start.5 = (f32[2,128,128]{2,1,0:T(8,128)S(1)}, f32[2,128,128]{2,1,0:T(8,128)}, u32[]{:S(2)}) copy-start(f32[2,128,128]{2,1,0:T(8,128)} %get-tuple-element.61.refs_0_) | copy-start | bytes 393220
  122.5 0.9 copy-start.14
  129.6 21.2 %all-to-all-start.1 = ((f32[32,1,128]{2,1,0:T(1,128)}), f32[32,1,128]{2,1,0:T(1,128)S(1)}, u32[]{:S(2)}, u32[]{:S(2)}) async-start(f32[32,1,128]{2,1,0:T(1,128)} %get-tuple-element.67), calls=%async_computation.1 | async-start | bytes 32768 | tf_op jit(solution)/shard_map/all_to_all | solution.py:547
  150.7 4.5 %copy-start.15 = (f32[2,128,128]{2,1,0:T(8,128)S(1)}, f32[2,128,128]{2,1,0:T(8,128)}, u32[]{:S(2)}) copy-start(f32[2,128,128]{2,1,0:T(8,128)} %get-tuple-element.64.refs_1_.later_ref) | copy-start | bytes 393220
  150.7 4.5 %copy-start.16 = (f32[2,128,128]{2,1,0:T(8,128)S(1)}, f32[2,128,128]{2,1,0:T(8,128)}, u32[]{:S(2)}) copy-start(f32[2,128,128]{2,1,0:T(8,128)} %get-tuple-element.92.last_ref) | copy-start | bytes 393220
  155.2 9.6 %copy-start.9 = (bf16[256,256]{1,0:T(8,128)(2,1)S(1)}, bf16[256,256]{1,0:T(8,128)(2,1)}, u32[]{:S(2)}) copy-start(bf16[256,256]{1,0:T(8,128)(2,1)} %copy-done.8) | copy-start | bytes 393220
  155.2 9.6 %copy-start.12 = (bf16[256,256]{1,0:T(8,128)(2,1)S(1)}, bf16[256,256]{1,0:T(8,128)(2,1)}, u32[]{:S(2)}) copy-start(bf16[256,256]{1,0:T(8,128)(2,1)} %copy-done.11) | copy-start | bytes 393220
  157.5 16.0 %all-to-all-start.2 = ((f32[8,32,128]{2,1,0:T(8,128)}), f32[8,32,128]{2,1,0:T(8,128)S(1)}, u32[]{:S(2)}, u32[]{:S(2)}) async-start(f32[8,32,128]{2,1,0:T(8,128)} %bitcast.10), calls=%async_computation.2 | async-start | bytes 262144 | tf_op jit(solution)/shard_map/all_to_all | solution.py:449
  163.3 47.0 %collective-permute-start.6 = (bf16[2,8,32,128]{3,2,1,0:T(8,128)(2,1)}, bf16[2,8,32,128]{3,2,1,0:T(8,128)(2,1)S(1)}, u32[]{:S(2)}, u32[]{:S(2)}) collective-permute-start(bf16[2,8,32,128]{3,2,1,0:T(8,128)(2,1)} %get-tuple-element.71), channel_id=1, source_target_pairs={{0,1},{1,0},{2,3},{3,2},{4,5},{5,4},{6,7},{7,6},{8,9},{9,8},{10,11... | collective-permute-start | bytes 393224 | tf_op jit(solution)/shard_map/ppermute | solution.py:443
  164.8 1.6 copy-start.7
  170.2 0.8 copy-start.2
  171.0 48.5 %collective-permute-start.15 = (bf16[2,24,32,128]{3,2,1,0:T(8,128)(2,1)}, bf16[2,24,32,128]{3,2,1,0:T(8,128)(2,1)}, u32[]{:S(2)}, u32[]{:S(2)}) collective-permute-start(bf16[2,24,32,128]{3,2,1,0:T(8,128)(2,1)} %get-tuple-element.85), channel_id=1, source_target_pairs={{0,2},{1,3},{2,0},{3,1},{4,6},{5,7},{6,4},{7,5},{8,10},{9,11},{10,... | collective-permute-start | bytes 1179656 | tf_op jit(solution)/shard_map/ppermute | solution.py:443
  173.5 9.7 %collective-permute-start.18 = (f32[32,128]{1,0:T(8,128)S(1)}, f32[32,128]{1,0:T(8,128)S(1)}, u32[]{:S(2)}, u32[]{:S(2)}) collective-permute-start(f32[32,128]{1,0:T(8,128)S(1)} %reduce_sum.19), channel_id=1, source_target_pairs={{0,1},{1,0},{2,3},{3,2},{4,5},{5,4},{6,7},{7,6},{8,9},{9,8},{10,11... | collective-permute-start | bytes 49160 | tf_op jit(solution)/shard_map/ppermute | solution.py:443
  174.1 21.7 %collective-permute-start.19 = (f32[32,128]{1,0:T(8,128)S(1)}, f32[32,128]{1,0:T(8,128)S(1)}, u32[]{:S(2)}, u32[]{:S(2)}) collective-permute-start(f32[32,128]{1,0:T(8,128)S(1)} %reduce_sum.19), channel_id=1, source_target_pairs={{0,2},{1,3},{2,0},{3,1},{4,6},{5,7},{6,4},{7,5},{8,10},{9,11},{10,... | collective-permute-start | bytes 49160 | tf_op jit(solution)/shard_map/ppermute | solution.py:443
  174.6 24.2 %collective-permute-start.20 = (f32[32,128]{1,0:T(8,128)S(1)}, f32[32,128]{1,0:T(8,128)S(1)}, u32[]{:S(2)}, u32[]{:S(2)}) collective-permute-start(f32[32,128]{1,0:T(8,128)S(1)} %reduce_sum.19), channel_id=1, source_target_pairs={{0,3},{1,2},{2,1},{3,0},{4,7},{5,6},{6,5},{7,4},{8,11},{9,10},{10,... | collective-permute-start | bytes 49160 | tf_op jit(solution)/shard_map/ppermute | solution.py:443
  178.0 1.6 copy-start.1
  183.2 27.9 %collective-permute-start.7 = (bf16[2,8,32,128]{3,2,1,0:T(8,128)(2,1)}, bf16[2,8,32,128]{3,2,1,0:T(8,128)(2,1)}, u32[]{:S(2)}, u32[]{:S(2)}) collective-permute-start(bf16[2,8,32,128]{3,2,1,0:T(8,128)(2,1)} %get-tuple-element.72), channel_id=1, source_target_pairs={{0,2},{1,3},{2,0},{3,1},{4,6},{5,7},{6,4},{7,5},{8,10},{9,11},{10,... | collective-permute-start | bytes 393224 | tf_op jit(solution)/shard_map/ppermute | solution.py:443
  195.7 15.4 %collective-permute-start.8 = (bf16[2,8,32,128]{3,2,1,0:T(8,128)(2,1)}, bf16[2,8,32,128]{3,2,1,0:T(8,128)(2,1)}, u32[]{:S(2)}, u32[]{:S(2)}) collective-permute-start(bf16[2,8,32,128]{3,2,1,0:T(8,128)(2,1)} %get-tuple-element.73), channel_id=1, source_target_pairs={{0,3},{1,2},{2,1},{3,0},{4,7},{5,6},{6,5},{7,4},{8,11},{9,10},{10,... | collective-permute-start | bytes 393224 | tf_op jit(solution)/shard_map/ppermute | solution.py:443
  199.5 20.0 %all-to-all-start.3 = ((f32[8,32,128]{2,1,0:T(8,128)}), f32[8,32,128]{2,1,0:T(8,128)}, u32[]{:S(2)}, u32[]{:S(2)}) async-start(f32[8,32,128]{2,1,0:T(8,128)} %broadcast_in_dim.8), calls=%async_computation.3 | async-start | bytes 262144 | tf_op jit(solution)/shard_map/all_to_all | solution.py:459
  203.7 1.6 copy-start
  208.4 1.8 copy-start.3
  208.4 2.7 %copy-start.6 = (bf16[256,4096]{1,0:T(8,128)(2,1)S(1)}, bf16[256,4096]{1,0:T(8,128)(2,1)}, u32[]{:S(2)}) copy-start(bf16[256,4096]{1,0:T(8,128)(2,1)} %get-tuple-element.69.col_ref.col_hbm) | copy-start | bytes 6291460
  208.4 2.7 %copy-start.10 = (bf16[256,256]{1,0:T(8,128)(2,1)S(1)}, bf16[256,256]{1,0:T(8,128)(2,1)}, u32[]{:S(2)}) copy-start(bf16[256,256]{1,0:T(8,128)(2,1)} %copy-done.8) | copy-start | bytes 393220
  208.4 2.8 %copy-start.13 = (bf16[256,256]{1,0:T(8,128)(2,1)S(1)}, bf16[256,256]{1,0:T(8,128)(2,1)}, u32[]{:S(2)}) copy-start(bf16[256,256]{1,0:T(8,128)(2,1)} %copy-done.11) | copy-start | bytes 393220
  210.2 40.4 %collective-permute-start.16 = (bf16[2,40,32,128]{3,2,1,0:T(8,128)(2,1)S(1)}, bf16[2,40,32,128]{3,2,1,0:T(8,128)(2,1)}, u32[]{:S(2)}, u32[]{:S(2)}) collective-permute-start(bf16[2,40,32,128]{3,2,1,0:T(8,128)(2,1)S(1)} %copy-done.3), channel_id=1, source_target_pairs={{0,1},{1,0},{2,3},{3,2},{4,5},{5,4},{6,7},{7,6},{8,9},{9,8},{10,11... | collective-permute-start | bytes 1966088 | tf_op jit(solution)/shard_map/ppermute | solution.py:443
  210.3 42.4 %collective-permute-start.17 = (bf16[2,24,32,128]{3,2,1,0:T(8,128)(2,1)S(1)}, bf16[2,24,32,128]{3,2,1,0:T(8,128)(2,1)}, u32[]{:S(2)}, u32[]{:S(2)}) collective-permute-start(bf16[2,24,32,128]{3,2,1,0:T(8,128)(2,1)S(1)} %get-tuple-element.88), channel_id=1, source_target_pairs={{0,3},{1,2},{2,1},{3,0},{4,7},{5,6},{6,5},{7,4},{8,11},{9,10},{10,... | collective-permute-start | bytes 1179656 | tf_op jit(solution)/shard_map/ppermute | solution.py:443
  215.9 2.6 copy-start.4
  215.9 33.2 %collective-permute-start.9 = (bf16[2,24,32,128]{3,2,1,0:T(8,128)(2,1)}, bf16[2,24,32,128]{3,2,1,0:T(8,128)(2,1)}, u32[]{:S(2)}, u32[]{:S(2)}) collective-permute-start(bf16[2,24,32,128]{3,2,1,0:T(8,128)(2,1)} %get-tuple-element.74), channel_id=1, source_target_pairs={{0,2},{1,3},{2,0},{3,1},{4,6},{5,7},{6,4},{7,5},{8,10},{9,11},{10,... | collective-permute-start | bytes 1179656 | tf_op jit(solution)/shard_map/ppermute | solution.py:443
  218.5 48.2 %collective-permute-start.10 = (bf16[2,40,32,128]{3,2,1,0:T(8,128)(2,1)S(1)}, bf16[2,40,32,128]{3,2,1,0:T(8,128)(2,1)}, u32[]{:S(2)}, u32[]{:S(2)}) collective-permute-start(bf16[2,40,32,128]{3,2,1,0:T(8,128)(2,1)S(1)} %get-tuple-element.76), channel_id=1, source_target_pairs={{0,1},{1,0},{2,3},{3,2},{4,5},{5,4},{6,7},{7,6},{8,9},{9,8},{10,11... | collective-permute-start | bytes 1966088 | tf_op jit(solution)/shard_map/ppermute | solution.py:443
  219.5 49.3 %collective-permute-start.11 = (bf16[2,24,32,128]{3,2,1,0:T(8,128)(2,1)}, bf16[2,24,32,128]{3,2,1,0:T(8,128)(2,1)S(1)}, u32[]{:S(2)}, u32[]{:S(2)}) collective-permute-start(bf16[2,24,32,128]{3,2,1,0:T(8,128)(2,1)} %copy-done.4), channel_id=1, source_target_pairs={{0,3},{1,2},{2,1},{3,0},{4,7},{5,6},{6,5},{7,4},{8,11},{9,10},{10,... | collective-permute-start | bytes 1179656 | tf_op jit(solution)/shard_map/ppermute | solution.py:443
  253.8 16.8 %copy-start.19 = (bf16[2,128,32,128]{3,2,1,0:T(8,128)(2,1)}, bf16[2,128,32,128]{3,2,1,0:T(8,128)(2,1)S(1)}, u32[]{:S(2)}) copy-start(bf16[2,128,32,128]{3,2,1,0:T(8,128)(2,1)S(1)} %constant_dynamic-update-slice_fusion) | copy-start | bytes 6291460
  268.8 1.7 copy-start.18
  (3 other events, 2.2 us)
